TPU v7x, 512 devices: a 8x2x16 block of a 8x8x16 slice. The times are simulated.
512 devices in a mesh: body: 2 (over y), gx: 16 (over z), gy: 8 (over x), gz: 2 (over core).
Axes of the slice: x: 8, y: 2, z: 16, core: 2. Of those that a mesh axis runs over, the one named last changes fastest.
The devices are a block of a 8x8x16 slice.
Arguments:
- fields: float32 [4, 3, 64, 64, 256], P('body', None, 'gx', 'gy', 'gz'), parts along dimension 0, may hold values from -0.06 to 0.06
- macro_strain: float32 [6, 3], P('body'), parts along dimension 0, may hold values from -0.15 to 0.15
- material: float32 [4], P('body'), parts along dimension 0, may hold values from 2 to 10
Outputs:
- residual: float32 [6, 64, 64, 256], P('body', 'gx', 'gy', 'gz'), parts along dimension 0
- tangent: float32 [6, 64, 64, 256], P('body', 'gx', 'gy', 'gz'), parts along dimension 0
- stats: float32 [4], P('body'), parts along dimension 0
There are 2 independent parts, one for each index of `body`. A program takes and returns all parts, laid end to end along the dimension named above; each array names one. Nothing has to cross between parts.
All inputs are finite; a program needn't handle non-finite values.
Results may differ from a plain program's by a relative error of at most 0.0002.
Values sent between devices are 32-bit elements; how exact they have to be, the bound alone decides.
A program may use at most 64 MiB of HBM per device.

v0:
```python
import functools
import math

import jax
import jax.numpy as jnp
import numpy as np
from jax import lax
from jax.sharding import PartitionSpec as P

highest = lax.Precision.HIGHEST
spacing = 4.0
root_eps = 1e-06


def passed_along(block, axis, distance):
    devices = range(lax.axis_size(axis))
    route = [((i - distance) % len(devices), i) for i in devices]
    return lax.ppermute(block, axis, route)


def one_axis_at_a_time(x, axes):
    return functools.reduce(lax.psum, axes, x)


def shape_tables():
    gauss_root = math.sqrt(0.6)
    points = np.array([-gauss_root, 0.0, gauss_root])
    values = np.stack(
        [points * (points - 1.0) / 2.0, 1.0 - points * points, points * (points + 1.0) / 2.0],
        axis=1,
    )
    slopes = np.stack([points - 0.5, -2.0 * points, points + 0.5], axis=1) * (2.0 / spacing)
    weights = np.array([5.0 / 9.0, 8.0 / 9.0, 5.0 / 9.0])
    volume = (
        weights[:, None, None]
        * weights[None, :, None]
        * weights[None, None, :]
        * (spacing / 2.0) ** 3
    )
    return (
        jnp.asarray(values, jnp.float32),
        jnp.asarray(slopes, jnp.float32),
        jnp.asarray(volume, jnp.float32),
    )


def triplets(array, axis):
    elements = (array.shape[axis] - 1) // 2
    even_nodes = lax.slice_in_dim(array, 0, 2 * elements, 2, axis)
    odd_nodes = lax.slice_in_dim(array, 1, 2 * elements, 2, axis)
    next_nodes = lax.slice_in_dim(array, 2, 2 * elements + 1, 2, axis)
    return jnp.stack([even_nodes, odd_nodes, next_nodes], axis=2)


def scatter_back(stacked):
    pieces = [lax.index_in_dim(stacked, slot_index, 2, keepdims=False) for slot_index in range(3)]
    pad_after = [(0, 0)] * pieces[0].ndim
    pad_after[3] = (0, 1)
    pad_before = [(0, 0)] * pieces[0].ndim
    pad_before[3] = (1, 0)
    even_nodes = jnp.pad(pieces[0], pad_after) + jnp.pad(pieces[2], pad_before)
    odd_nodes = jnp.pad(pieces[1], pad_after)
    paired = jnp.stack([even_nodes, odd_nodes], axis=4)
    merged_shape = paired.shape[:3] + (2 * paired.shape[3],) + paired.shape[5:]
    merged = paired.reshape(merged_shape)
    return lax.slice_in_dim(merged, 0, merged.shape[3] - 1, 1, 3)


def stresses(grads, strain, shear, lame_first):
    deform = [
        [
            grads[col_at][row_at] + strain[row_at, col_at] + (1.0 if row_at == col_at else 0.0)
            for col_at in range(3)
        ]
        for row_at in range(3)
    ]
    change = [[grads[col_at][3 + row_at] for col_at in range(3)] for row_at in range(3)]
    cofactor = [
        [
            deform[(row_at + 1) % 3][(col_at + 1) % 3] * deform[(row_at + 2) % 3][(col_at + 2) % 3]
            - deform[(row_at + 1) % 3][(col_at + 2) % 3]
            * deform[(row_at + 2) % 3][(col_at + 1) % 3]
            for col_at in range(3)
        ]
        for row_at in range(3)
    ]
    volume_ratio = (
        deform[0][0] * cofactor[0][0]
        + deform[0][1] * cofactor[0][1]
        + deform[0][2] * cofactor[0][2]
    )
    inverse_t = [
        [cofactor[row_at][col_at] / volume_ratio for col_at in range(3)] for row_at in range(3)
    ]
    log_ratio = jnp.log(volume_ratio)
    stress = [
        [
            shear * (deform[row_at][col_at] - inverse_t[row_at][col_at])
            + lame_first * log_ratio * inverse_t[row_at][col_at]
            for col_at in range(3)
        ]
        for row_at in range(3)
    ]
    trace_term = sum(
        (
            inverse_t[row_at][col_at] * change[row_at][col_at]
            for row_at in range(3)
            for col_at in range(3)
        )
    )
    product = [
        [
            sum((inverse_t[row_at][mid_at] * change[col_at][mid_at] for mid_at in range(3)))
            for col_at in range(3)
        ]
        for row_at in range(3)
    ]
    twisted = [
        [
            sum((product[row_at][mid_at] * inverse_t[mid_at][col_at] for mid_at in range(3)))
            for col_at in range(3)
        ]
        for row_at in range(3)
    ]
    softening = shear - lame_first * log_ratio
    dstress = [
        [
            shear * change[row_at][col_at]
            + softening * twisted[row_at][col_at]
            + lame_first * trace_term * inverse_t[row_at][col_at]
            for col_at in range(3)
        ]
        for row_at in range(3)
    ]
    return (stress, dstress)


def layer_forces(slab_nodes, strain, material):
    values, slopes, volume = shape_tables()
    grid_stack = triplets(triplets(slab_nodes, 3), 3)
    grid_shape = grid_stack.shape
    stacked = grid_stack.reshape(grid_shape[:4] + (1, grid_shape[4] * grid_shape[5]))
    z_value = jnp.einsum("qa,cxyaij->cxyqij", values, stacked, precision=highest)
    z_slope = jnp.einsum("qa,cxyaij->cxyqij", slopes, stacked, precision=highest)
    y_value = jnp.einsum("qa,cxazij->cxqzij", values, z_value, precision=highest)
    y_slope = jnp.einsum("qa,cxazij->cxqzij", slopes, z_value, precision=highest)
    yz_slope = jnp.einsum("qa,cxazij->cxqzij", values, z_slope, precision=highest)
    grads = [
        jnp.einsum("qa,cayzij->cqyzij", slopes, y_value, precision=highest),
        jnp.einsum("qa,cayzij->cqyzij", values, y_slope, precision=highest),
        jnp.einsum("qa,cayzij->cqyzij", values, yz_slope, precision=highest),
    ]
    stress, dstress = stresses(grads, strain, material[0], material[1])
    weight = volume[:, :, :, None, None]
    fluxes = [
        jnp.stack(
            [
                stress[0][along],
                stress[1][along],
                stress[2][along],
                dstress[0][along],
                dstress[1][along],
                dstress[2][along],
            ]
        )
        * weight
        for along in range(3)
    ]
    back_x0 = jnp.einsum("qa,cqyzij->cayzij", slopes, fluxes[0], precision=highest)
    back_x1 = jnp.einsum("qa,cqyzij->cayzij", values, fluxes[1], precision=highest)
    back_x2 = jnp.einsum("qa,cqyzij->cayzij", values, fluxes[2], precision=highest)
    back_y = jnp.einsum("qa,cxqzij->cxazij", values, back_x0, precision=highest) + jnp.einsum(
        "qa,cxqzij->cxazij", slopes, back_x1, precision=highest
    )
    back_yz = jnp.einsum("qa,cxqzij->cxazij", values, back_x2, precision=highest)
    back_z = jnp.einsum("qa,cxyqij->cxyaij", values, back_y, precision=highest) + jnp.einsum(
        "qa,cxyqij->cxyaij", slopes, back_yz, precision=highest
    )
    return scatter_back(scatter_back(back_z.reshape(grid_shape)))


def assemble(nodes, macro_strain, material):
    layers = (nodes.shape[1] - 1) // 2

    def one_layer(layer_index, accumulated):
        plane_start = (2 * layer_index).astype(jnp.int32)
        slab_nodes = lax.dynamic_slice_in_dim(nodes, plane_start, 3, 1)
        contribution = layer_forces(slab_nodes, macro_strain, material)
        current = lax.dynamic_slice_in_dim(accumulated, plane_start, 3, 1)
        return lax.dynamic_update_slice_in_dim(accumulated, current + contribution, plane_start, 1)

    return lax.fori_loop(0, layers, one_layer, jnp.zeros(nodes.shape, jnp.float32))


def fold_upper(accumulated, spilled, axis):
    first = lax.slice_in_dim(accumulated, 0, 1, 1, axis) + spilled
    middle = lax.slice_in_dim(accumulated, 1, accumulated.shape[axis] - 1, 1, axis)
    return jnp.concatenate([first, middle], axis=axis)


def local(fields, macro_strain, material):
    flat = fields.reshape((6,) + fields.shape[2:])
    nodes = flat
    upper = passed_along(nodes[:, :1], "gx", -1)
    nodes = jnp.concatenate([nodes, upper], axis=1)
    upper = passed_along(nodes[:, :, :1], "gy", -1)
    nodes = jnp.concatenate([nodes, upper], axis=2)
    upper = passed_along(nodes[:, :, :, :1], "gz", -1)
    nodes = jnp.concatenate([nodes, upper], axis=3)
    accumulated = assemble(nodes, macro_strain, material)
    spilled = passed_along(accumulated[:, :, :, -1:], "gz", 1)
    accumulated = fold_upper(accumulated, spilled, 3)
    spilled = passed_along(accumulated[:, :, -1:], "gy", 1)
    accumulated = fold_upper(accumulated, spilled, 2)
    spilled = passed_along(accumulated[:, -1:], "gx", 1)
    owned = fold_upper(accumulated, spilled, 1)
    residual = owned[:3]
    tangent = owned[3:]
    squares = jnp.sum(residual * residual)
    curvature = jnp.sum(flat[3:] * tangent)
    totals = (
        one_axis_at_a_time(squares, ("gx", "gy", "gz")),
        one_axis_at_a_time(curvature, ("gx", "gy", "gz")),
    )
    entries = (
        3.0
        * flat.shape[1]
        * flat.shape[2]
        * flat.shape[3]
        * lax.axis_size("gx")
        * lax.axis_size("gy")
        * lax.axis_size("gz")
    )
    stats = jnp.stack([jnp.sqrt(totals[0] / entries + root_eps), totals[1] / entries])
    return (residual, tangent, stats)


def solution(mesh):
    in_specs = (P("body", None, "gx", "gy", "gz"), P("body", None), P("body"))
    out_specs = (P("body", "gx", "gy", "gz"), P("body", "gx", "gy", "gz"), P("body"))
    return jax.shard_map(local, mesh=mesh, in_specs=in_specs, out_specs=out_specs, check_vma=False)
```

profile of v0, /device:TPU:65, one launch (start us, length us, event | category | flops | bytes accessed | tf_op | source)
XLA Modules:
  0.0 261.3 jit_solution(14529519410099005642)
XLA Ops:
  0.7 0.9 copy.88
  1.6 44.6 %collective-permute-start = (f32[6,1,8,128]{3,2,0,1:T(8,128)S(1)}, f32[6,1,8,128]{3,2,0,1:T(8,128)S(1)}, u32[]{:S(2)}, u32[]{:S(2)}) collective-permute-start(f32[6,1,8,128]{3,2,0,1:T(8,128)S(1)} %slice.599), channel_id=1, source_target_pairs={{16,0},{32,16},{48,32},{64,48},{80,64},{96,80},{112,96},{128,112},... | collective-permute-start | bytes 73736 | tf_op jit(solution)/shard_map/ppermute | solution.py:18
  46.2 0.9 collective-permute-done
  47.1 5.5 %collective-permute-start.1 = (f32[6,5,1,128]{3,2,0,1:T(1,128)S(1)}, f32[6,5,1,128]{3,2,0,1:T(1,128)S(1)}, u32[]{:S(2)}, u32[]{:S(2)}) collective-permute-start(f32[6,5,1,128]{3,2,0,1:T(1,128)S(1)} %pad_maximum_fusion.8), channel_id=1, source_target_pairs={{2,0},{4,2},{6,4},{8,6},{10,8},{12,10},{14,12},{0,14},{3,1},{5,3},... | collective-permute-start | bytes 46088 | tf_op jit(solution)/shard_map/ppermute | solution.py:18
  52.6 0.8 collective-permute-done.1
  53.5 4.3 %collective-permute-start.2 = (f32[6,5,9,1]{3,2,0,1:T(8,128)S(1)}, f32[6,5,9,1]{3,2,0,1:T(8,128)S(1)}, u32[]{:S(2)}, u32[]{:S(2)}) collective-permute-start(f32[6,5,9,1]{3,2,0,1:T(8,128)S(1)} %pad_maximum_fusion.4), channel_id=1, source_target_pairs={{1,0},{0,1},{3,2},{2,3},{5,4},{4,5},{7,6},{6,7},{9,8},{8,9},{11,10... | collective-permute-start | bytes 3248 | tf_op jit(solution)/shard_map/ppermute | solution.py:18
  57.7 1.1 collective-permute-done.2
  59.0 130.9 %while.16 = (s32[]{:T(128)}, f32[6,5,9,129]{3,2,1,0:T(8,128)S(1)}, f32[2]{0:T(128)S(1)}, f32[6,5,9,129]{3,2,0,1:T(8,128)S(1)}, f32[3,3]{1,0:T(4,128)S(1)}, /*ind...) while((s32[]{:T(128)}, f32[6,5,9,129]{3,2,1,0:T(8,128)S(1)}, ...), condition=%wide.region_1.2_spmd.clone, body=%wide.region_0.1_spmd.sunk.clone.sunk | while | flops 26604940 | bytes 19892932 | solution.py:192
  59.0 0.8 copy-done
  59.8 1.7 slice.981
  61.6 1.7 slice.982
  63.3 1.7 slice.983
  71.8 7.0 %constant_dynamic-update-slice_fusion.35 = (f32[6,3,3,3,256]{4,1,3,2,0:T(4,128)S(1)}, f32[1,3,3,3,1,256]{5,1,3,2,4,0:T(4,128)S(1)}, f32[1,3,3,3,1,256]{5,1,3,2,4...) fusion(f32[]{:T(128)} %bitcast.376, f32[]{:T(128)} %bitcast.377, ...), kind=kLoop, calls=%fused_computation.67.clone.1 | loop fusion | flops 221183 | bytes 433196 | tf_op jit(solution)/shard_map/while
  78.7 4.4 %constant_dynamic-update-slice_fusion.36 = (f32[6,3,3,3,256]{4,1,3,2,0:T(4,128)S(1)}, f32[1,3,3,3,1,256]{5,1,3,2,4,0:T(4,128)S(1)}) fusion(f32[6,3,3,3,256]{4,1,3,2,0:T(4,128)S(1)} %get-tuple-element.388, f32[]{:T(128)} %bitcast.376, f32[]{:T(128)} %bitcast.388, f32[6,3,3,3,1,256]{5,1,3,2,4,0:T(4,128)S(1)} %convolution_bitcast_fusion.24, ...), kind=kLoop, calls=%fused_computation.66.clone.1 | loop fusion | flops 103680 | bytes 294940 | tf_op jit(solution)/shard_map/while
  83.1 4.5 %constant_dynamic-update-slice_fusion.37 = (f32[6,3,3,3,256]{4,1,3,2,0:T(4,128)S(1)}, f32[1,3,3,3,1,256]{5,1,3,2,4,0:T(4,128)S(1)}) fusion(f32[6,3,3,3,256]{4,1,3,2,0:T(4,128)S(1)} %get-tuple-element.390, f32[]{:T(128)} %bitcast.376, f32[]{:T(128)} %bitcast.385, f32[6,3,3,3,1,256]{5,1,3,2,4,0:T(4,128)S(1)} %convolution_bitcast_fusion.24, ...), kind=kLoop, calls=%fused_computation.65.clone.1 | loop fusion | flops 117504 | bytes 294940 | tf_op jit(solution)/shard_map/while
  87.7 7.1 %constant_dynamic-update-slice_fusion.38 = (f32[6,3,3,3,256]{4,1,3,2,0:T(4,128)S(1)}, f32[1,3,3,3,1,256]{5,1,3,2,4,0:T(4,128)S(1)}, f32[1,3,3,3,1,256]{5,1,3,2,4...) fusion(f32[6,3,3,3,256]{4,1,3,2,0:T(4,128)S(1)} %get-tuple-elem, ...), kind=kLoop, calls=%fused_computation.64.clone.1 | loop fusion | flops 483840 | bytes 1290284 | tf_op jit(solution)/shard_map/while
  94.8 1.4 constant_dynamic-update-slice_fusion.43
  96.2 1.4 constant_dynamic-update-slice_fusion.45
  97.6 1.9 constant_dynamic-update-slice_fusion.39
  99.5 1.9 constant_dynamic-update-slice_fusion.40
  101.5 1.9 constant_dynamic-update-slice_fusion.41
  103.4 2.0 constant_dynamic-update-slice_fusion.42
  105.4 2.0 constant_dynamic-update-slice_fusion.44
  107.4 2.0 constant_dynamic-update-slice_fusion.46
  109.5 1.4 constant_dynamic-update-slice_fusion.47
  110.8 1.4 constant_dynamic-update-slice_fusion.48
  112.2 1.4 constant_dynamic-update-slice_fusion.49
  119.0 0.8 copy.184
  119.8 0.8 reshape.1083
  121.1 1.2 slice_add_fusion.13
  122.4 2.0 copy.185
  124.5 0.8 copy-done
  125.3 1.7 slice.981
  127.0 1.7 slice.982
  128.7 1.7 slice.983
  137.2 7.0 %constant_dynamic-update-slice_fusion.35 = (f32[6,3,3,3,256]{4,1,3,2,0:T(4,128)S(1)}, f32[1,3,3,3,1,256]{5,1,3,2,4,0:T(4,128)S(1)}, f32[1,3,3,3,1,256]{5,1,3,2,4...) fusion(f32[]{:T(128)} %bitcast.376, f32[]{:T(128)} %bitcast.377, ...), kind=kLoop, calls=%fused_computation.67.clone.1 | loop fusion | flops 221183 | bytes 433196 | tf_op jit(solution)/shard_map/while
  144.2 4.4 %constant_dynamic-update-slice_fusion.36 = (f32[6,3,3,3,256]{4,1,3,2,0:T(4,128)S(1)}, f32[1,3,3,3,1,256]{5,1,3,2,4,0:T(4,128)S(1)}) fusion(f32[6,3,3,3,256]{4,1,3,2,0:T(4,128)S(1)} %get-tuple-element.388, f32[]{:T(128)} %bitcast.376, f32[]{:T(128)} %bitcast.388, f32[6,3,3,3,1,256]{5,1,3,2,4,0:T(4,128)S(1)} %convolution_bitcast_fusion.24, ...), kind=kLoop, calls=%fused_computation.66.clone.1 | loop fusion | flops 103680 | bytes 294940 | tf_op jit(solution)/shard_map/while
  148.6 4.5 %constant_dynamic-update-slice_fusion.37 = (f32[6,3,3,3,256]{4,1,3,2,0:T(4,128)S(1)}, f32[1,3,3,3,1,256]{5,1,3,2,4,0:T(4,128)S(1)}) fusion(f32[6,3,3,3,256]{4,1,3,2,0:T(4,128)S(1)} %get-tuple-element.390, f32[]{:T(128)} %bitcast.376, f32[]{:T(128)} %bitcast.385, f32[6,3,3,3,1,256]{5,1,3,2,4,0:T(4,128)S(1)} %convolution_bitcast_fusion.24, ...), kind=kLoop, calls=%fused_computation.65.clone.1 | loop fusion | flops 117504 | bytes 294940 | tf_op jit(solution)/shard_map/while
  153.1 7.1 %constant_dynamic-update-slice_fusion.38 = (f32[6,3,3,3,256]{4,1,3,2,0:T(4,128)S(1)}, f32[1,3,3,3,1,256]{5,1,3,2,4,0:T(4,128)S(1)}, f32[1,3,3,3,1,256]{5,1,3,2,4...) fusion(f32[6,3,3,3,256]{4,1,3,2,0:T(4,128)S(1)} %get-tuple-elem, ...), kind=kLoop, calls=%fused_computation.64.clone.1 | loop fusion | flops 483840 | bytes 1290284 | tf_op jit(solution)/shard_map/while
  160.2 1.4 constant_dynamic-update-slice_fusion.43
  161.6 1.4 constant_dynamic-update-slice_fusion.45
  163.0 1.9 constant_dynamic-update-slice_fusion.39
  165.0 1.9 constant_dynamic-update-slice_fusion.40
  166.9 1.9 constant_dynamic-update-slice_fusion.41
  168.8 2.0 constant_dynamic-update-slice_fusion.42
  170.9 2.0 constant_dynamic-update-slice_fusion.44
  172.9 2.0 constant_dynamic-update-slice_fusion.46
  174.9 1.4 constant_dynamic-update-slice_fusion.47
  176.3 1.4 constant_dynamic-update-slice_fusion.48
  177.6 1.4 constant_dynamic-update-slice_fusion.49
  184.4 0.8 copy.184
  185.2 0.8 reshape.1083
  186.6 1.2 slice_add_fusion.13
  187.8 2.0 copy.185
  189.9 2.3 collective-permute-start.3
  192.4 1.0 collective-permute-done.3
  193.5 2.0 collective-permute-start.4
  195.5 4.3 %collective-permute-done.4 = f32[6,5,1,128]{3,2,1,0:T(1,128)S(1)} collective-permute-done((f32[6,5,1,128]{3,2,1,0:T(1,128)S(1)}, f32[6,5,1,128]{3,2,1,0:T(1,128)S(1)}, u32[]{:S(2)}, u32[]{:S(2)}) %collective-permute-start.4) | collective-permute-done | bytes 15392 | tf_op jit(solution)/shard_map/ppermute | solution.py:18
  200.0 2.0 collective-permute-start.5
  202.0 4.4 %collective-permute-done.5 = f32[6,1,8,128]{3,2,1,0:T(8,128)S(1)} collective-permute-done((f32[6,1,8,128]{3,2,1,0:T(8,128)S(1)}, f32[6,1,8,128]{3,2,1,0:T(8,128)S(1)}, u32[]{:S(2)}, u32[]{:S(2)}) %collective-permute-start.5) | collective-permute-done | bytes 24608 | tf_op jit(solution)/shard_map/ppermute | solution.py:18
  206.4 1.3 fusion.33
  207.7 22.4 %all-reduce.6 = (f32[]{:T(128)}, f32[]{:T(128)}) all-reduce(f32[]{:T(128)} %get-tuple-element.268, f32[]{:T(128)} %get-tuple-element.294), channel_id=1, replica_groups=mesh['body'=2,'gx'=16,'gy'=8,'gz'=2] {'gx'}, use_global_device_ids=true, to_apply=%region_7.8 | all-reduce | flops 2 | bytes 16 | tf_op jit(solution)/shard_map/psum | solution.py:22
  230.2 12.8 %all-reduce.7 = (f32[]{:T(128)}, f32[]{:T(128)}) all-reduce(f32[]{:T(128)} %get-tuple-element.234, f32[]{:T(128)} %get-tuple-element.235), channel_id=1, replica_groups=mesh['body'=2,'gx'=16,'gy'=8,'gz'=2] {'gy'}, use_global_device_ids=true, to_apply=%region_8.9 | all-reduce | flops 2 | bytes 16 | tf_op jit(solution)/shard_map/psum | solution.py:22
  242.9 16.4 %all-reduce.8 = (f32[]{:T(128)}, f32[]{:T(128)}) all-reduce(f32[]{:T(128)} %get-tuple-element.236, f32[]{:T(128)} %get-tuple-element.237), channel_id=1, replica_groups=mesh['body'=2,'gx'=16,'gy'=8,'gz'=2] {'gz'}, use_global_device_ids=true, to_apply=%region_9.10 | all-reduce | flops 2 | bytes 16 | tf_op jit(solution)/shard_map/psum | solution.py:22
  (121 shorter events, 26.2 us)
Async XLA Ops:
  0.6 58.3 %copy-start.2 = (f32[3,3,1,1,1]{1,0,4,3,2:T(4,128)S(1)}, f32[3,3,1,1,1]{1,0,4,3,2:T(4,128)}, u32[]{:S(2)}) copy-start(f32[3,3,1,1,1]{1,0,4,3,2:T(4,128)} %constant.293) | copy-start | bytes 112
  0.6 58.3 %copy-start.4 = (f32[3,3,1,1,1]{1,0,4,3,2:T(4,128)S(1)}, f32[3,3,1,1,1]{1,0,4,3,2:T(4,128)}, u32[]{:S(2)}) copy-start(f32[3,3,1,1,1]{1,0,4,3,2:T(4,128)} %constant.294) | copy-start | bytes 112
  0.7 58.3 %copy-start.3 = (f32[3,3,3]{0,2,1:T(4,128)S(1)}, f32[3,3,3]{0,2,1:T(4,128)}, u32[]{:S(2)}) copy-start(f32[3,3,3]{0,2,1:T(4,128)} %constant.74.clone..sunk.2) | copy-start | bytes 328
  0.7 58.3 %copy-start.7 = (f32[2]{0:T(128)S(1)}, f32[2]{0:T(128)}, u32[]{:S(2)}) copy-start(f32[2]{0:T(128)} %param.10) | copy-start | bytes 28
  0.7 58.3 %copy-start.5 = (f32[3,3]{1,0:T(4,128)S(1)}, f32[3,3]{1,0:T(4,128)}, u32[]{:S(2)}) copy-start(f32[3,3]{1,0:T(4,128)} %param.9) | copy-start | bytes 112
  1.6 45.5 %collective-permute-start = (f32[6,1,8,128]{3,2,0,1:T(8,128)S(1)}, f32[6,1,8,128]{3,2,0,1:T(8,128)S(1)}, u32[]{:S(2)}, u32[]{:S(2)}) collective-permute-start(f32[6,1,8,128]{3,2,0,1:T(8,128)S(1)} %slice.599), channel_id=1, source_target_pairs={{16,0},{32,16},{48,32},{64,48},{80,64},{96,80},{112,96},{128,112},... | collective-permute-start | bytes 73736 | tf_op jit(solution)/shard_map/ppermute | solution.py:18
  47.1 6.3 %collective-permute-start.1 = (f32[6,5,1,128]{3,2,0,1:T(1,128)S(1)}, f32[6,5,1,128]{3,2,0,1:T(1,128)S(1)}, u32[]{:S(2)}, u32[]{:S(2)}) collective-permute-start(f32[6,5,1,128]{3,2,0,1:T(1,128)S(1)} %pad_maximum_fusion.8), channel_id=1, source_target_pairs={{2,0},{4,2},{6,4},{8,6},{10,8},{12,10},{14,12},{0,14},{3,1},{5,3},... | collective-permute-start | bytes 46088 | tf_op jit(solution)/shard_map/ppermute | solution.py:18
  53.5 5.4 %collective-permute-start.2 = (f32[6,5,9,1]{3,2,0,1:T(8,128)S(1)}, f32[6,5,9,1]{3,2,0,1:T(8,128)S(1)}, u32[]{:S(2)}, u32[]{:S(2)}) collective-permute-start(f32[6,5,9,1]{3,2,0,1:T(8,128)S(1)} %pad_maximum_fusion.4), channel_id=1, source_target_pairs={{1,0},{0,1},{3,2},{2,3},{5,4},{4,5},{7,6},{6,7},{9,8},{8,9},{11,10... | collective-permute-start | bytes 3248 | tf_op jit(solution)/shard_map/ppermute | solution.py:18
  59.0 0.8 copy-start
  122.4 2.1 copy-start.1
  124.5 0.8 copy-start
  187.8 2.1 copy-start.1
  189.9 3.4 %collective-permute-start.3 = (f32[6,5,9,1]{3,2,1,0:T(8,128)S(1)}, f32[6,5,9,1]{3,2,1,0:T(8,128)S(1)}, u32[]{:S(2)}, u32[]{:S(2)}) collective-permute-start(f32[6,5,9,1]{3,2,1,0:T(8,128)S(1)} %slice.478), channel_id=1, source_target_pairs={{1,0},{0,1},{3,2},{2,3},{5,4},{4,5},{7,6},{6,7},{9,8},{8,9},{11,10... | collective-permute-start | bytes 3248 | tf_op jit(solution)/shard_map/ppermute | solution.py:18
  192.4 14.0 %copy-start.6 = (f32[2,3,4,8,128]{4,3,2,1,0:T(8,128)S(1)}, f32[2,3,4,8,128]{4,3,2,1,0:T(8,128)}, u32[]{:S(2)}) copy-start(f32[2,3,4,8,128]{4,3,2,1,0:T(8,128)} %param.8) | copy-start | bytes 294916
  193.5 6.3 %collective-permute-start.4 = (f32[6,5,1,128]{3,2,1,0:T(1,128)S(1)}, f32[6,5,1,128]{3,2,1,0:T(1,128)S(1)}, u32[]{:S(2)}, u32[]{:S(2)}) collective-permute-start(f32[6,5,1,128]{3,2,1,0:T(1,128)S(1)} %pad_maximum_fusion.7), channel_id=1, source_target_pairs={{14,0},{0,2},{2,4},{4,6},{6,8},{8,10},{10,12},{12,14},{15,1},{1,3}... | collective-permute-start | bytes 46088 | tf_op jit(solution)/shard_map/ppermute | solution.py:18
  200.0 6.4 %collective-permute-start.5 = (f32[6,1,8,128]{3,2,1,0:T(8,128)S(1)}, f32[6,1,8,128]{3,2,1,0:T(8,128)S(1)}, u32[]{:S(2)}, u32[]{:S(2)}) collective-permute-start(f32[6,1,8,128]{3,2,1,0:T(8,128)S(1)} %slice.601), channel_id=1, source_target_pairs={{240,0},{0,16},{16,32},{32,48},{48,64},{64,80},{80,96},{96,112},{1... | collective-permute-start | bytes 73736 | tf_op jit(solution)/shard_map/ppermute | solution.py:18
where the time goes:
time: 263 us; the launch traced here: 261 us
  other arithmetic  88.9 us (34%)
  starting transfers between devices  60.5 us (23%)
  blocking collectives  51.6 us (20%)
  local copies, waits for them, and re-layouts  27.5 us (10%)
  matrix products  17.2 us (7%)
  waiting for transfers between devices  12.6 us (5%)
    while x24, other arithmetic  73.9 us
    ppermute x6, starting transfers between devices, passed_along(): return lax.ppermute(block, axis, route)  60.5 us
    psum x3, blocking collectives, one_axis_at_a_time(): return functools.reduce(lax.psum, axes, x)  51.6 us
    ppermute x6, waiting for transfers between devices, passed_along(): return lax.ppermute(block, axis, route)  12.6 us
    another operation x6, other arithmetic, layer_forces(): jnp.stack([stress[0][along], stress[1][along], stress[2][along], dstress[...  9.6 us
  transfers between devices with their start and end apart: 6, of which 6 were waited for; matrix products, arithmetic and copies ran while one was open for 0% of the time, Pallas kernels for 0%

commit v1 on v0

v1 whole, which is shorter than its diff:
```python
import functools
import math

import jax
import jax.numpy as jnp
import numpy as np
from jax import lax
from jax.experimental import pallas as pl
from jax.experimental.pallas import tpu as pltpu
from jax.sharding import PartitionSpec as P

MESH = pl.DeviceIdType.MESH
spacing = 4.0
root_eps = 1e-06
f32 = jnp.float32
bf16 = jnp.bfloat16


def tables():
    root = math.sqrt(0.6)
    points = np.array([-root, 0.0, root])
    values = np.stack(
        [points * (points - 1.0) / 2.0, 1.0 - points * points, points * (points + 1.0) / 2.0], axis=1
    )
    slopes = np.stack([points - 0.5, -2.0 * points, points + 0.5], axis=1) * (2.0 / spacing)
    weights = np.array([5.0 / 9.0, 8.0 / 9.0, 5.0 / 9.0]) * (spacing / 2.0)
    return values, slopes, weights


def ceil_to(n, m):
    return -(-n // m) * m


class Layout:
    def __init__(self, nx, ny, nz):
        self.nx, self.ny, self.nz = nx, ny, nz
        self.own = nx * ny
        self.xm = self.own
        self.xp = self.xm + 2 * ny
        self.ym_own = self.xp + ny
        self.ym_xm = self.ym_own + 2 * nx
        self.ym_xp = self.ym_xm + 4
        self.yp_own = self.ym_xp + 2
        self.yp_xm = self.yp_own + nx
        self.yp_xp = self.yp_xm + 2
        self.used = self.yp_xp + 1
        self.rows = ceil_to(self.used, 16)
        self.ex, self.ey, self.ez = nx // 2 + 1, ny // 2 + 1, nz // 2 + 1
        self.group = ceil_to(self.ex * self.ey, 16)
        self.points = 9 * self.group
        self.lanes = ceil_to(3 * self.ez, 128)

    def row(self, p, r):
        if 0 <= r < self.ny:
            if 0 <= p < self.nx:
                return p * self.ny + r
            if p < 0:
                return self.xm + (p + 2) * self.ny + r
            return self.xp + r
        if r < 0:
            if 0 <= p < self.nx:
                return self.ym_own + 2 * p + r + 2
            if p < 0:
                return self.ym_xm + 2 * (p + 2) + r + 2
            return self.ym_xp + r + 2
        if 0 <= p < self.nx:
            return self.yp_own + p
        if p < 0:
            return self.yp_xm + p + 2
        return self.yp_xp


def split_np(a):
    a = a.astype(np.float32)
    high = np.asarray(a, dtype=jnp.bfloat16)
    low = np.asarray(a - high.astype(np.float32), dtype=jnp.bfloat16)
    return high, low


def matrices(lay):
    values, slopes, weights = tables()
    forward = np.zeros((3, lay.points, lay.rows))
    back = np.zeros((3, lay.own, lay.points))
    pairs = ((slopes, values), (values, slopes), (values, values))
    for kind, (tx, ty) in enumerate(pairs):
        for q1 in range(3):
            for q2 in range(3):
                for ex in range(lay.ex):
                    for ey in range(lay.ey):
                        point = (q1 * 3 + q2) * lay.group + ex * lay.ey + ey
                        for a1 in range(3):
                            for a2 in range(3):
                                p, r = 2 * (ex - 1) + a1, 2 * (ey - 1) + a2
                                factor = tx[q1, a1] * ty[q2, a2]
                                forward[kind, point, lay.row(p, r)] += factor
                                if 0 <= p < lay.nx and 0 <= r < lay.ny:
                                    back[kind, p * lay.ny + r, point] += factor * weights[q1] * weights[q2]
    along_z = np.zeros((2, 2 * lay.nz, lay.lanes))
    z_back = np.zeros((2, lay.lanes, lay.nz))
    for kind, tz in enumerate((values, slopes)):
        for q3 in range(3):
            for ez in range(lay.ez):
                for a3 in range(3):
                    z = 2 * (ez - 1) + a3
                    column = q3 * lay.ez + ez
                    if z < 0:
                        k = lay.nz + lay.nz + z
                    elif z >= lay.nz:
                        k = lay.nz + z - lay.nz
                    else:
                        k = z
                        z_back[kind, column, z] += tz[q3, a3] * weights[q3]
                    along_z[kind, k, column] += tz[q3, a3]
    along_z = np.concatenate([along_z[0], along_z[1]], axis=1)
    fh, fl = split_np(forward)
    forward = np.concatenate([fh, fh, fl], axis=2)
    bh, bl = split_np(back)
    back = np.concatenate([bh, bl], axis=1)
    along_z = np.stack(split_np(along_z))
    z_back = np.stack(split_np(z_back), axis=1)
    return forward, back, along_z, z_back


def split(x):
    high = x.astype(bf16)
    return high, (x - high.astype(f32)).astype(bf16)


def dot(a, b):
    return jnp.dot(a, b, preferred_element_type=f32)


def kernel(
    lay, sizes,
    fields, strain, material, forward_h, back_h, along_h, z_back_h,
    residual_h, tangent_h, stats,
    ext, extp, forward, back, along, z_back, grads, flux, out, send_a, recv_a, send_b, recv_b,
    load_sem, const_sem, halo_send, halo_recv, core_send, core_recv, out_sem,
    a_send, a_recv, b_send, b_recv, far_sem,
):
    n = dict(sizes)
    me = {axis: lax.axis_index(axis) for axis in ("gx", "gy", "gz")}
    nx, ny, nz = lay.nx, lay.ny, lay.nz

    def device(**shifts):
        return {
            axis: lax.rem(me[axis] + (shift % n[axis]), n[axis]) for axis, shift in shifts.items()
        }

    load = pltpu.make_async_copy(fields, ext.at[:, 0 : lay.own, :], load_sem)
    load.start()

    barrier = pltpu.get_barrier_semaphore()
    near = (device(gz=1), device(gx=1), device(gx=-1), device(gy=1), device(gy=-1))
    for where in near:
        pl.semaphore_signal(barrier, inc=1, device_id=where, device_id_type=MESH)

    constants = [
        pltpu.make_async_copy(source, target, const_sem.at[i])
        for i, (source, target) in enumerate(
            ((along_h, along), (forward_h, forward), (back_h, back), (z_back_h, z_back))
        )
    ]
    for copy in constants:
        copy.start()
    tail = lay.rows - lay.used
    if tail:
        ext[:, lay.used :, :] = jnp.zeros((6, tail, nz), f32)

    count = [0]
    sends = []

    def send(source, target, where):
        i = count[0]
        count[0] += 1
        copy = pltpu.make_async_remote_copy(
            src_ref=ext.at[:, source[0] : source[0] + source[1], :],
            dst_ref=ext.at[:, target : target + source[1], :],
            send_sem=halo_send.at[i],
            recv_sem=halo_recv.at[i],
            device_id=where,
            device_id_type=MESH,
        )
        copy.start()
        sends.append(copy)

    load.wait()
    pl.semaphore_wait(barrier, len(near))
    send(((nx - 2) * ny, 2 * ny), lay.xm, device(gx=1))
    send((0, ny), lay.xp, device(gx=-1))
    for p in range(nx):
        send((p * ny + ny - 2, 2), lay.ym_own + 2 * p, device(gy=1))
        send((p * ny, 1), lay.yp_own + p, device(gy=-1))
    to_core = device(gz=1)
    core_own = pltpu.make_async_remote_copy(
        src_ref=ext.at[:, 0 : lay.own, :],
        dst_ref=extp.at[:, 0 : lay.own, :],
        send_sem=core_send.at[0],
        recv_sem=core_recv.at[0],
        device_id=to_core,
        device_id_type=MESH,
    )
    core_own.start()

    def greet(step):
        d = 2**step
        for where in (device(gx=d), device(gx=-d), device(gy=d), device(gy=-d)):
            pl.semaphore_signal(far_sem.at[step], inc=1, device_id=where, device_id_type=MESH)

    rounds = 1
    while 2**rounds < n["gx"] // 2 or 2**rounds <= n["gy"] // 2:
        rounds += 1
    greet(0)
    pl.semaphore_wait(far_sem.at[0], 4)
    for p in range(2):
        send(((nx - 2 + p) * ny + ny - 2, 2), lay.ym_xm + 2 * p, device(gx=1, gy=1))
        send(((nx - 2 + p) * ny, 1), lay.yp_xm + p, device(gx=1, gy=-1))
    send((ny - 2, 2), lay.ym_xp, device(gx=-1, gy=1))
    send((0, 1), lay.yp_xp, device(gx=-1, gy=-1))
    for step in range(1, rounds):
        greet(step)
        if step < rounds - 1:
            pl.semaphore_wait(far_sem.at[step], 4)

    for copy in sends:
        copy.wait()
    core_halo = pltpu.make_async_remote_copy(
        src_ref=ext.at[:, lay.own :, :],
        dst_ref=extp.at[:, lay.own :, :],
        send_sem=core_send.at[1],
        recv_sem=core_recv.at[1],
        device_id=to_core,
        device_id_type=MESH,
    )
    core_halo.start()
    for copy in constants:
        copy.wait()
    core_own.wait()
    core_halo.wait()

    lanes = lay.lanes
    for c in range(6):
        nodes = jnp.concatenate([ext[c], extp[c]], axis=1)
        high, low = split(nodes)
        z = dot(high, along[0]) + dot(low, along[0]) + dot(high, along[1])
        vh, vl = split(z[:, :lanes])
        sh, sl = split(z[:, lanes:])
        value = jnp.concatenate([vh, vl, vh], axis=0)
        slope = jnp.concatenate([sh, sl, sh], axis=0)
        grads[c, 0] = dot(forward[0], value)
        grads[c, 1] = dot(forward[1], value)
        grads[c, 2] = dot(forward[2], slope)

    shear, lame = material[0], material[1]
    ratio = lame / shear
    shift = [
        [strain[i, j] + (1.0 if i == j else 0.0) for j in range(3)] for i in range(3)
    ]

    def points(i, carry):
        for half in range(lanes // 128):
            at = (pl.ds(pl.multiple_of(i * 8, 8), 8), pl.ds(half * 128, 128))
            f = [[grads[(r, c) + at] + shift[r][c] for c in range(3)] for r in range(3)]
            dv = [[grads[(3 + r, c) + at] for c in range(3)] for r in range(3)]
            cof = [
                [
                    f[(r + 1) % 3][(c + 1) % 3] * f[(r + 2) % 3][(c + 2) % 3]
                    - f[(r + 1) % 3][(c + 2) % 3] * f[(r + 2) % 3][(c + 1) % 3]
                    for c in range(3)
                ]
                for r in range(3)
            ]
            det = f[0][0] * cof[0][0] + f[0][1] * cof[0][1] + f[0][2] * cof[0][2]
            inverse = 1.0 / det
            g = [[cof[r][c] * inverse for c in range(3)] for r in range(3)]
            pressure = ratio * jnp.log(det) - 1.0
            for r in range(3):
                for c in range(3):
                    flux[(r, c) + at] = f[r][c] + pressure * g[r][c]
            m = [
                [g[r][0] * dv[c][0] + g[r][1] * dv[c][1] + g[r][2] * dv[c][2] for c in range(3)]
                for r in range(3)
            ]
            trace = ratio * (m[0][0] + m[1][1] + m[2][2])
            w = [
                [trace - pressure * m[r][c] if r == c else -(pressure * m[r][c]) for c in range(3)]
                for r in range(3)
            ]
            for r in range(3):
                for c in range(3):
                    flux[(3 + r, c) + at] = dv[r][c] + (
                        w[r][0] * g[0][c] + w[r][1] * g[1][c] + w[r][2] * g[2][c]
                    )
        return carry

    lax.fori_loop(0, lay.points // 8, points, 0)

    own = lay.own
    squares = jnp.zeros((8, nz), f32)
    curvature = jnp.zeros((8, nz), f32)
    for c in range(6):
        def plane(kind, along_axis):
            high, low = split(flux[c, along_axis])
            both = dot(back[kind], high)
            return both[:own] + both[own:] + dot(back[kind, :own], low)

        vh, vl = split(plane(0, 0) + plane(1, 1))
        sh, sl = split(plane(2, 2))
        result = (
            dot(vh, z_back[0, 0]) + dot(vl, z_back[0, 0]) + dot(vh, z_back[0, 1])
            + dot(sh, z_back[1, 0]) + dot(sl, z_back[1, 0]) + dot(sh, z_back[1, 1])
        ) * shear
        out[c] = result
        product = result * result if c < 3 else result * ext[c, :own]
        part = product[0:8]
        for k in range(1, own // 8):
            part = part + product[8 * k : 8 * k + 8]
        if c < 3:
            squares = squares + part
        else:
            curvature = curvature + part

    writes = [
        pltpu.make_async_copy(out.at[0:3], residual_h, out_sem.at[0]),
        pltpu.make_async_copy(out.at[3:6], tangent_h, out_sem.at[1]),
    ]
    for copy in writes:
        copy.start()

    if rounds > 1:
        pl.semaphore_wait(far_sem.at[rounds - 1], 4)

    def exchange(totals, partners, sending, receiving, send_sems, recv_sems):
        sending[...] = totals
        copies = []
        for slot, where in enumerate(partners):
            copy = pltpu.make_async_remote_copy(
                src_ref=sending,
                dst_ref=receiving.at[slot],
                send_sem=send_sems.at[slot],
                recv_sem=recv_sems.at[slot],
                device_id=where,
                device_id_type=MESH,
            )
            copy.start()
            copies.append(copy)
        for copy in copies:
            copy.wait()
        return totals + jnp.sum(receiving[...], axis=0)

    totals = jnp.concatenate(
        [jnp.sum(squares, axis=0, keepdims=True), jnp.sum(curvature, axis=0, keepdims=True)], axis=0
    )
    half = n["gx"] // 2
    order = [k for d in range(half, 0, -1) for k in sorted({d, n["gx"] - d})]
    totals = exchange(
        totals, [device(gx=k) for k in order], send_a, recv_a, a_send, a_recv
    )
    half = n["gy"] // 2
    order = [k for d in range(half, 0, -1) for k in sorted({d, n["gy"] - d})] + [0]
    partners = []
    for k in order:
        partners.append(device(gy=k, gz=1))
        if k:
            partners.append(device(gy=k))
    totals = exchange(totals, partners, send_b, recv_b, b_send, b_recv)

    sums = jnp.sum(totals, axis=1, keepdims=True)
    entries = 3.0 * nx * ny * nz * n["gx"] * n["gy"] * n["gz"]
    means = sums / entries
    root = jnp.sqrt(means + root_eps)
    stats[0] = root[0, 0]
    stats[1] = means[1, 0]
    for copy in writes:
        copy.wait()


def solution(mesh):
    sizes = tuple((axis, mesh.shape[axis]) for axis in ("gx", "gy", "gz"))
    n = dict(sizes)

    def local(fields, macro_strain, material):
        nx, ny, nz = fields.shape[2:]
        lay = Layout(nx, ny, nz)
        consts = [jnp.asarray(m) for m in matrices(lay)]
        hbm = pl.BlockSpec(memory_space=pltpu.HBM)
        smem = pl.BlockSpec(memory_space=pltpu.SMEM)
        halos = 2 + 2 * nx + 6
        block = jax.ShapeDtypeStruct((3, lay.own, nz), f32)
        n_a, n_b = n["gx"] - 1, n["gy"] * n["gz"] - 1
        dma = pltpu.SemaphoreType.DMA
        residual, tangent, stats = pl.pallas_call(
            functools.partial(kernel, lay, sizes),
            out_shape=(block, block, jax.ShapeDtypeStruct((2,), f32)),
            in_specs=[hbm, smem, smem, hbm, hbm, hbm, hbm],
            out_specs=(hbm, hbm, smem),
            scratch_shapes=[
                pltpu.VMEM((6, lay.rows, nz), f32),
                pltpu.VMEM((6, lay.rows, nz), f32),
                *[pltpu.VMEM(m.shape, bf16) for m in consts],
                pltpu.VMEM((6, 3, lay.points, lay.lanes), f32),
                pltpu.VMEM((6, 3, lay.points, lay.lanes), f32),
                pltpu.VMEM((6, lay.own, nz), f32),
                pltpu.VMEM((2, nz), f32),
                pltpu.VMEM((n_a, 2, nz), f32),
                pltpu.VMEM((2, nz), f32),
                pltpu.VMEM((n_b, 2, nz), f32),
                dma,
                dma((4,)),
                dma((halos,)),
                dma((halos,)),
                dma((2,)),
                dma((2,)),
                dma((2,)),
                dma((n_a,)),
                dma((n_a,)),
                dma((n_b,)),
                dma((n_b,)),
                pltpu.SemaphoreType.REGULAR((8,)),
            ],
            compiler_params=pltpu.CompilerParams(collective_id=0, has_side_effects=True),
            name="cell",
        )(fields.reshape(6, nx * ny, nz), macro_strain, material, *consts)
        shape = (3, nx, ny, nz)
        return residual.reshape(shape), tangent.reshape(shape), stats

    in_specs = (P("body", None, "gx", "gy", "gz"), P("body", None), P("body"))
    out_specs = (P("body", "gx", "gy", "gz"), P("body", "gx", "gy", "gz"), P("body"))
    return jax.shard_map(local, mesh=mesh, in_specs=in_specs, out_specs=out_specs, check_vma=False)
```

time: 263 us -> 72.8 us (0.28)
  other arithmetic: 88.9 us -> 0 us
  Pallas kernels: 0 us -> 69.3 us
  starting transfers between devices: 60.5 us -> 0 us
  blocking collectives: 51.6 us -> 0 us
  local copies, waits for them, and re-layouts: 27.5 us -> 2.61 us
  matrix products: 17.2 us -> 0 us
  waiting for transfers between devices: 12.6 us -> 0 us
    while x24 -> x0, other arithmetic: 73.9 us -> none
    pallas_call x0 -> x1, Pallas kernels: none -> 69.3 us  [local(): pl.pallas_call(functools.partial(kernel, lay, sizes), out_shape=(block, b...]
    ppermute x6 -> x0, starting transfers between devices: 60.5 us -> none  [passed_along(): return lax.ppermute(block, axis, route)]
    psum x3 -> x0, blocking collectives: 51.6 us -> none  [one_axis_at_a_time(): return functools.reduce(lax.psum, axes, x)]
    dot_general x32 -> x0, matrix products: 17.2 us -> none  [the longest x2 1.19 us: layer_forces(): jnp.einsum('qa,cqyzij->cayzij', values, fluxes[2], precision=highest)]
    slice x21 -> x0, local copies, waits for them, and re-layouts: 14.8 us -> none  [the longest x4 4.04 us: triplets(): next_nodes = lax.slice_in_dim(array, 2, 2 * elements + 1, 2, axis)]
    ppermute x6 -> x0, waiting for transfers between devices: 12.6 us -> none  [passed_along(): return lax.ppermute(block, axis, route)]
    another operation x17 -> x0, other arithmetic: 10.8 us -> none  [the longest x6 9.6 us: layer_forces(): jnp.stack([stress[0][along], stress[1][along], stress[2][along], dstress[...]
  transfers between devices with their start and end apart: 6 -> 0, of which waited for: 6 -> 0; matrix products, arithmetic and copies ran while one was open for 0% -> 0% of each run, Pallas kernels for 0% -> 0%
where the time goes in v1:
time: 72.8 us; the launch traced here: 72.6 us
  Pallas kernels  69.3 us (95%)
  local copies, waits for them, and re-layouts  2.61 us (4%)
    pallas_call x1, Pallas kernels, local(): pl.pallas_call(functools.partial(kernel, lay, sizes), out_shape=(block, b...  69.3 us
    unnamed x7, local copies, waits for them, and re-layouts  2.61 us

profile of v1, /device:TPU:65, one launch (start us, length us, event | category | flops | bytes accessed | tf_op | source)
XLA Modules:
  0.0 72.6 jit_solution(10651749216542685269)
XLA Ops:
  0.6 69.3 %cell.1 = (f32[3,32,128]{2,1,0:T(8,128)}, f32[3,32,128]{2,1,0:T(8,128)}, f32[2]{0:T(128)}) custom-call(f32[6,32,128]{2,1,0:T(8,128)} %bitcast.3, f32[3,3]{1,0:T(4,128)} %strain.1, f32[2]{0:T(128)} %material.1, bf16[3,144,240]{2,1,0:T(8,128)(2,1)} %constant.8.clone.forward_h, bf16[3,64,144]{2,1,0:T(8,128)(2,1)} %constant.9.clone.back_h, ...), custom_call_target="tpu_custom_call" | custom-call | tf_op jit(solution)/shard_map/cell/pallas_call | solution.py:392
  70.0 0.0 copy-start
  70.0 1.4 %copy.13 = f32[3,4,8,128]{3,2,1,0:T(8,128)} copy(f32[3,4,8,128]{3,2,1,0:T(8,128)} %bitcast.5) | data formatting | bytes 98304
  71.4 0.0 copy-done
  71.4 0.0 copy-start.1
  71.4 0.6 copy.14
  72.0 0.0 copy-done.1
  72.1 0.5 copy.15
Async XLA Ops:
  70.0 1.4 %copy-start = (f32[3,32,128]{2,1,0:T(8,128)S(1)}, f32[3,32,128]{2,1,0:T(8,128)}, u32[]{:S(2)}) copy-start(f32[3,32,128]{2,1,0:T(8,128)} %get-tuple-element.7) | copy-start | bytes 147460
  71.4 0.7 copy-start.1

commit v2 on v1

v2 whole, which is shorter than its diff:
```python
import functools
import math

import jax
import jax.numpy as jnp
import numpy as np
from jax import lax
from jax.experimental import pallas as pl
from jax.experimental.pallas import tpu as pltpu
from jax.sharding import PartitionSpec as P

MESH = pl.DeviceIdType.MESH
spacing = 4.0
root_eps = 1e-06
f32 = jnp.float32
bf16 = jnp.bfloat16


def tables():
    root = math.sqrt(0.6)
    points = np.array([-root, 0.0, root])
    values = np.stack(
        [points * (points - 1.0) / 2.0, 1.0 - points * points, points * (points + 1.0) / 2.0], axis=1
    )
    slopes = np.stack([points - 0.5, -2.0 * points, points + 0.5], axis=1) * (2.0 / spacing)
    weights = np.array([5.0 / 9.0, 8.0 / 9.0, 5.0 / 9.0]) * (spacing / 2.0)
    return values, slopes, weights


def ceil_to(n, m):
    return -(-n // m) * m


class Layout:
    def __init__(self, nx, ny, nz):
        self.nx, self.ny, self.nz = nx, ny, nz
        self.own = nx * ny
        self.xm = self.own
        self.xp = self.xm + 2 * ny
        self.ym_own = self.xp + ny
        self.ym_xm = self.ym_own + 2 * nx
        self.ym_xp = self.ym_xm + 4
        self.yp_own = self.ym_xp + 2
        self.yp_xm = self.yp_own + nx
        self.yp_xp = self.yp_xm + 2
        self.used = self.yp_xp + 1
        self.rows = ceil_to(self.used, 16)
        self.ex, self.ey, self.ez = nx // 2 + 1, ny // 2 + 1, nz // 2 + 1
        self.group = ceil_to(self.ex * self.ey, 16)
        self.points = 9 * self.group
        self.lanes = ceil_to(3 * self.ez, 128)

    def row(self, p, r):
        if 0 <= r < self.ny:
            if 0 <= p < self.nx:
                return p * self.ny + r
            if p < 0:
                return self.xm + (p + 2) * self.ny + r
            return self.xp + r
        if r < 0:
            if 0 <= p < self.nx:
                return self.ym_own + 2 * p + r + 2
            if p < 0:
                return self.ym_xm + 2 * (p + 2) + r + 2
            return self.ym_xp + r + 2
        if 0 <= p < self.nx:
            return self.yp_own + p
        if p < 0:
            return self.yp_xm + p + 2
        return self.yp_xp


def split_np(a):
    a = a.astype(np.float32)
    high = np.asarray(a, dtype=jnp.bfloat16)
    low = np.asarray(a - high.astype(np.float32), dtype=jnp.bfloat16)
    return high, low


def matrices(lay):
    values, slopes, weights = tables()
    forward = np.zeros((3, lay.points, lay.rows))
    back = np.zeros((3, lay.own, lay.points))
    pairs = ((slopes, values), (values, slopes), (values, values))
    for kind, (tx, ty) in enumerate(pairs):
        for q1 in range(3):
            for q2 in range(3):
                for ex in range(lay.ex):
                    for ey in range(lay.ey):
                        point = (q1 * 3 + q2) * lay.group + ex * lay.ey + ey
                        for a1 in range(3):
                            for a2 in range(3):
                                p, r = 2 * (ex - 1) + a1, 2 * (ey - 1) + a2
                                factor = tx[q1, a1] * ty[q2, a2]
                                forward[kind, point, lay.row(p, r)] += factor
                                if 0 <= p < lay.nx and 0 <= r < lay.ny:
                                    back[kind, p * lay.ny + r, point] += factor * weights[q1] * weights[q2]
    along_z = np.zeros((2, 2 * lay.nz, lay.lanes))
    z_back = np.zeros((2, lay.lanes, lay.nz))
    inside = [(q3, ez) for q3 in range(3) for ez in range(1, lay.ez - 1)]
    edge = [(q3, ez) for q3 in range(3) for ez in (0, lay.ez - 1)]
    for column, (q3, ez) in enumerate(inside + edge):
        for kind, tz in enumerate((values, slopes)):
            for a3 in range(3):
                z = 2 * (ez - 1) + a3
                if z < 0:
                    k = lay.nz + lay.nz + z
                elif z >= lay.nz:
                    k = lay.nz + z - lay.nz
                else:
                    k = z
                    z_back[kind, column, z] += tz[q3, a3] * weights[q3]
                along_z[kind, k, column] += tz[q3, a3]
    fh, fl = split_np(forward)
    forward = np.concatenate([fh, fh, fl], axis=2)
    bh, bl = split_np(back)
    back = np.concatenate([bh, bl], axis=1)
    first = np.concatenate(along_z[:, : lay.nz, :128], axis=1)
    second = np.concatenate(along_z[:, :, 128:], axis=1)
    first = np.concatenate(split_np(first), axis=0)
    second = np.stack(split_np(second))
    zh, zl = split_np(z_back)
    z_back = np.concatenate([zh, zl], axis=2)
    return forward, back, first, second, z_back


def split(x):
    high = x.astype(bf16)
    return high, (x - high.astype(f32)).astype(bf16)


def dot(a, b):
    return jnp.dot(a, b, preferred_element_type=f32)


def kernel(
    lay, sizes,
    fields, strain_h, material_h, forward_h, back_h, first_h, second_h, z_back_h,
    out, totals_ref,
    ext, extp, strain, material, forward, back, first, second, z_back, grads, flux, middle,
    send_a, recv_a, send_b, recv_b,
    load_sem, const_sem, halo_send, halo_recv, core_send, core_recv,
    a_send, a_recv, b_send, b_recv, far_sem,
):
    n = dict(sizes)
    me = {axis: lax.axis_index(axis) for axis in ("gx", "gy", "gz")}
    nx, ny, nz = lay.nx, lay.ny, lay.nz
    own, rows = lay.own, lay.rows

    def device(**shifts):
        return {
            axis: lax.rem(me[axis] + (shift % n[axis]), n[axis]) for axis, shift in shifts.items()
        }

    load = pltpu.make_async_copy(fields, ext.at[:, 0:own, :], load_sem)
    load.start()

    barrier = pltpu.get_barrier_semaphore()
    near = [device(gx=1), device(gx=-1), device(gy=1), device(gy=-1)]
    near += [device(gx=i, gy=j) for i in (1, -1) for j in (1, -1)] + [device(gz=1)]
    for where in near:
        pl.semaphore_signal(barrier, inc=1, device_id=where, device_id_type=MESH)

    constants = [
        pltpu.make_async_copy(source, target, const_sem.at[i])
        for i, (source, target) in enumerate(
            (
                (first_h, first), (forward_h, forward), (second_h, second), (back_h, back),
                (z_back_h, z_back), (strain_h, strain), (material_h, material),
            )
        )
    ]
    for copy in constants:
        copy.start()
    if rows > lay.used:
        ext[:, lay.used :, :] = jnp.zeros((6, rows - lay.used, nz), f32)

    count = [0]
    sends = []

    def send(source, target, where):
        i = count[0]
        count[0] += 1
        copy = pltpu.make_async_remote_copy(
            src_ref=ext.at[:, source[0] : source[0] + source[1], :],
            dst_ref=ext.at[:, target : target + source[1], :],
            send_sem=halo_send.at[i],
            recv_sem=halo_recv.at[i],
            device_id=where,
            device_id_type=MESH,
        )
        copy.start()
        sends.append(copy)

    load.wait()
    pl.semaphore_wait(barrier, len(near))
    send(((nx - 2) * ny, 2 * ny), lay.xm, device(gx=1))
    send((0, ny), lay.xp, device(gx=-1))
    for p in range(2):
        send(((nx - 2 + p) * ny + ny - 2, 2), lay.ym_xm + 2 * p, device(gx=1, gy=1))
        send(((nx - 2 + p) * ny, 1), lay.yp_xm + p, device(gx=1, gy=-1))
    send((ny - 2, 2), lay.ym_xp, device(gx=-1, gy=1))
    send((0, 1), lay.yp_xp, device(gx=-1, gy=-1))
    for p in range(nx):
        send((p * ny + ny - 2, 2), lay.ym_own + 2 * p, device(gy=1))
        send((p * ny, 1), lay.yp_own + p, device(gy=-1))

    def to_core(i, start, stop):
        return pltpu.make_async_remote_copy(
            src_ref=ext.at[:, start:stop, :],
            dst_ref=extp.at[:, start:stop, :],
            send_sem=core_send.at[i],
            recv_sem=core_recv.at[i],
            device_id=device(gz=1),
            device_id_type=MESH,
        )

    core_own = to_core(0, 0, own)
    core_own.start()

    def greet(step):
        d = 2**step
        for where in (device(gx=d), device(gx=-d), device(gy=d), device(gy=-d)):
            pl.semaphore_signal(far_sem.at[step], inc=1, device_id=where, device_id_type=MESH)

    far = 1
    while 2**far < n["gx"] // 2 or 2**far <= n["gy"] // 2:
        far += 1
    for step in range(far):
        greet(step)
        if step < far - 1:
            pl.semaphore_wait(far_sem.at[step], 4)

    for copy in sends:
        copy.wait()
    core_halo = to_core(1, own, rows)
    core_halo.start()
    for copy in constants:
        copy.wait()

    def to_points(tile, z):
        high, low = split(z)
        for pair in range(3):
            parts = []
            for kind in range(2):
                sides = []
                for c in (2 * pair, 2 * pair + 1):
                    at = (slice(c * rows, c * rows + rows), slice(kind * 128, kind * 128 + 128))
                    sides.append(jnp.concatenate([high[at], low[at], high[at]], axis=0))
                parts.append(jnp.concatenate(sides, axis=1))
            grads[tile, pair, 0] = dot(forward[0], parts[0])
            grads[tile, pair, 1] = dot(forward[1], parts[0])
            grads[tile, pair, 2] = dot(forward[2], parts[1])

    shear, lame = material[0], material[1]
    ratio = lame / shear
    shift = [
        [strain[i, j] + (1.0 if i == j else 0.0) for j in range(3)] for i in range(3)
    ]

    def stresses(tile):
        def points(i, carry):
            for half in range(2):
                block = pl.ds(pl.multiple_of(i * 16 + half * 8, 8), 8)

                def gradient(c, along):
                    return grads[tile, c // 2, along, block, (c % 2) * 128 : (c % 2) * 128 + 128]

                lanes = slice(tile * 128, tile * 128 + 128)
                f = [[gradient(r, c) + shift[r][c] for c in range(3)] for r in range(3)]
                dv = [[gradient(3 + r, c) for c in range(3)] for r in range(3)]
                cof = [
                    [
                        f[(r + 1) % 3][(c + 1) % 3] * f[(r + 2) % 3][(c + 2) % 3]
                        - f[(r + 1) % 3][(c + 2) % 3] * f[(r + 2) % 3][(c + 1) % 3]
                        for c in range(3)
                    ]
                    for r in range(3)
                ]
                det = f[0][0] * cof[0][0] + f[0][1] * cof[0][1] + f[0][2] * cof[0][2]
                inverse = 1.0 / det
                g = [[cof[r][c] * inverse for c in range(3)] for r in range(3)]
                pressure = ratio * jnp.log(det) - 1.0
                for r in range(3):
                    for c in range(3):
                        flux[r, c, block, lanes] = f[r][c] + pressure * g[r][c]
                m = [
                    [
                        g[r][0] * dv[c][0] + g[r][1] * dv[c][1] + g[r][2] * dv[c][2]
                        for c in range(3)
                    ]
                    for r in range(3)
                ]
                trace = ratio * (m[0][0] + m[1][1] + m[2][2])
                w = [
                    [
                        trace - pressure * m[r][c] if r == c else -(pressure * m[r][c])
                        for c in range(3)
                    ]
                    for r in range(3)
                ]
                for r in range(3):
                    for c in range(3):
                        flux[3 + r, c, block, lanes] = dv[r][c] + (
                            w[r][0] * g[0][c] + w[r][1] * g[1][c] + w[r][2] * g[2][c]
                        )
            return carry

        lax.fori_loop(0, lay.points // 16, points, 0)

    nodes = ext[...].reshape(6 * rows, nz)
    high, low = split(nodes)
    weights = first[0:nz]
    z = dot(
        jnp.concatenate([high, low], axis=1), jnp.concatenate([weights, weights], axis=0)
    ) + dot(high, first[nz:])
    to_points(0, z)
    stresses(0)

    core_own.wait()
    core_halo.wait()
    nodes = jnp.concatenate([nodes, extp[...].reshape(6 * rows, nz)], axis=1)
    high, low = split(nodes)
    z = dot(high, second[0]) + dot(low, second[0]) + dot(high, second[1])
    to_points(1, z)
    stresses(1)

    for c in range(6):
        def plane(kind, along):
            high, low = split(flux[c, along])
            both = dot(back[kind], high)
            return both[:own] + both[own:] + dot(back[kind, :own], low)

        at = slice(c * own, c * own + own)
        for kind, part in enumerate((plane(0, 0) + plane(1, 1), plane(2, 2))):
            high, low = split(part)
            middle[kind, 0, at] = high
            middle[kind, 1, at] = low
    result = dot(middle[0, 1], z_back[0, :, :nz]) + dot(middle[1, 1], z_back[1, :, :nz])
    both = dot(middle[0, 0], z_back[0]) + dot(middle[1, 0], z_back[1])
    result = (result + both[:, :nz] + both[:, nz:]) * shear
    out[...] = result
    sums = []
    for c0 in (0, 3):
        total = jnp.zeros((8, nz), f32)
        for c in range(c0, c0 + 3):
            part = result[c * own : c * own + own]
            product = part * (part if c < 3 else ext[c, :own])
            for k in range(own // 8):
                total = total + product[8 * k : 8 * k + 8]
        sums.append(jnp.sum(total, axis=0, keepdims=True))
    totals = jnp.concatenate(sums, axis=0)

    pl.semaphore_wait(far_sem.at[far - 1], 4)

    def exchange(totals, partners, sending, receiving, send_sems, recv_sems):
        sending[...] = totals
        copies = []
        for slot, where in enumerate(partners):
            copy = pltpu.make_async_remote_copy(
                src_ref=sending,
                dst_ref=receiving.at[slot],
                send_sem=send_sems.at[slot],
                recv_sem=recv_sems.at[slot],
                device_id=where,
                device_id_type=MESH,
            )
            copy.start()
            copies.append(copy)
        for copy in copies:
            copy.wait_recv()
        return totals + jnp.sum(receiving[...], axis=0), copies

    half = n["gx"] // 2
    order = [k for d in range(1, half + 1) for k in sorted({d, n["gx"] - d})]
    totals, copies_a = exchange(
        totals, [device(gx=k) for k in order], send_a, recv_a, a_send, a_recv
    )
    half = n["gy"] // 2
    order = [k for d in range(half, 0, -1) for k in sorted({d, n["gy"] - d})] + [0]
    partners = []
    for k in order:
        partners.append(device(gy=k, gz=1))
        if k:
            partners.append(device(gy=k))
    totals, copies_b = exchange(totals, partners, send_b, recv_b, b_send, b_recv)
    totals_ref[...] = totals
    for copy in copies_a + copies_b:
        copy.wait_send()


def finish(entries, out, totals, residual, tangent, stats, held, sems):
    half = out.shape[0] // 2
    copies = [
        pltpu.make_async_copy(out.at[0:half], residual, sems.at[0]),
        pltpu.make_async_copy(out.at[half:], tangent, sems.at[1]),
    ]
    for copy in copies:
        copy.start()
    means = jnp.sum(totals[...], axis=1, keepdims=True) / entries
    root = jnp.sqrt(means + root_eps)
    held[0] = root[0, 0]
    held[1] = means[1, 0]
    copies.append(pltpu.make_async_copy(held, stats, sems.at[2]))
    copies[-1].start()
    for copy in copies:
        copy.wait()


def solution(mesh):
    sizes = tuple((axis, mesh.shape[axis]) for axis in ("gx", "gy", "gz"))
    n = dict(sizes)

    def local(fields, macro_strain, material):
        nx, ny, nz = fields.shape[2:]
        lay = Layout(nx, ny, nz)
        consts = [jnp.asarray(m) for m in matrices(lay)]
        hbm = pl.BlockSpec(memory_space=pltpu.HBM)
        vmem = pl.BlockSpec(memory_space=pltpu.VMEM)
        halos = 2 + 2 * nx + 6
        own = lay.own
        n_a, n_b = n["gx"] - 1, n["gy"] * n["gz"] - 1
        dma = pltpu.SemaphoreType.DMA
        out, totals = pl.pallas_call(
            functools.partial(kernel, lay, sizes),
            out_shape=(
                pltpu.VMEM((6 * own, nz), f32),
                pltpu.VMEM((2, nz), f32),
            ),
            in_specs=[hbm] * 8,
            out_specs=(vmem, vmem),
            scratch_shapes=[
                pltpu.VMEM((6, lay.rows, nz), f32),
                pltpu.VMEM((6, lay.rows, nz), f32),
                pltpu.SMEM(macro_strain.shape, f32),
                pltpu.SMEM(material.shape, f32),
                *[pltpu.VMEM(m.shape, bf16) for m in consts],
                pltpu.VMEM((2, 3, 3, lay.points, 256), f32),
                pltpu.VMEM((6, 3, lay.points, lay.lanes), f32),
                pltpu.VMEM((2, 2, 6 * own, lay.lanes), bf16),
                pltpu.VMEM((2, nz), f32),
                pltpu.VMEM((n_a, 2, nz), f32),
                pltpu.VMEM((2, nz), f32),
                pltpu.VMEM((n_b, 2, nz), f32),
                dma,
                dma((7,)),
                dma((halos,)),
                dma((halos,)),
                dma((2,)),
                dma((2,)),
                dma((n_a,)),
                dma((n_a,)),
                dma((n_b,)),
                dma((n_b,)),
                pltpu.SemaphoreType.REGULAR((8,)),
            ],
            compiler_params=pltpu.CompilerParams(
                collective_id=0, has_side_effects=True
            ),
            name="cell",
        )(fields.reshape(6, nx * ny, nz), macro_strain, material, *consts)
        entries = 3.0 * nx * ny * nz * n["gx"] * n["gy"] * n["gz"]
        block = jax.ShapeDtypeStruct((3 * own, nz), f32)
        residual, tangent, stats = pl.pallas_call(
            functools.partial(finish, entries),
            out_shape=(block, block, jax.ShapeDtypeStruct((2,), f32)),
            in_specs=[vmem, vmem],
            out_specs=(hbm, hbm, hbm),
            scratch_shapes=[pltpu.SMEM((2,), f32), dma((3,))],
            compiler_params=pltpu.CompilerParams(vmem_limit_bytes=24 * 2**20),
            name="finish",
        )(out, totals)
        shape = (3, nx, ny, nz)
        return residual.reshape(shape), tangent.reshape(shape), stats

    in_specs = (P("body", None, "gx", "gy", "gz"), P("body", None), P("body"))
    out_specs = (P("body", "gx", "gy", "gz"), P("body", "gx", "gy", "gz"), P("body"))
    return jax.shard_map(local, mesh=mesh, in_specs=in_specs, out_specs=out_specs, check_vma=False)
```

time: 72.8 us -> 67.6 us (0.929)
  local copies, waits for them, and re-layouts: 2.61 us -> 0 us
  Pallas kernels: 69.3 us -> 66.9 us
    unnamed x7 -> x0, local copies, waits for them, and re-layouts: 2.61 us -> none
    pallas_call x1 -> x2, Pallas kernels: 69.3 us -> 66.9 us  [the longest x1 66.2 us: local(): pl.pallas_call(functools.partial(kernel, lay, sizes), out_shape=(pltpu.VM...]
where the time goes in v2:
time: 67.6 us; the launch traced here: 67.5 us
  Pallas kernels  66.9 us (99%)
    pallas_call x1, Pallas kernels, local(): pl.pallas_call(functools.partial(kernel, lay, sizes), out_shape=(pltpu.VM...  66.2 us

profile of v2, /device:TPU:65, one launch (start us, length us, event | category | flops | bytes accessed | tf_op | source)
XLA Modules:
  0.0 67.5 jit_solution(7204573966015272630)
XLA Ops:
  0.6 66.2 %cell.1 = (f32[192,128]{1,0:T(8,128)S(1)}, f32[2,128]{1,0:T(2,128)S(1)}) custom-call(f32[6,32,128]{2,1,0:T(8,128)} %bitcast.3, f32[3,3]{1,0:T(4,128)} %strain_h.1, f32[2]{0:T(128)} %material_h.1, bf16[3,144,240]{2,1,0:T(8,128)(2,1)} %constant.10.clone.forward_h, bf16[3,64,144]{2,1,0:T(8,128)(2,1)} %constant.11.clone.back_h, ...), custom_call_target="tpu_custom_call" | custom-call | tf_op jit(solution)/shard_map/cell/pallas_call | solution.py:424
  66.8 0.7 finish.1

commit v3 on v2

--- a/solution.py
+++ b/solution.py
@@ -138,9 +138,9 @@
     fields, strain_h, material_h, forward_h, back_h, first_h, second_h, z_back_h,
     out, totals_ref,
     ext, extp, strain, material, forward, back, first, second, z_back, grads, flux, middle,
-    send_a, recv_a, send_b, recv_b,
+    own_row, plane_row, plane_rows, near_rows, far_rows,
     load_sem, const_sem, halo_send, halo_recv, core_send, core_recv,
-    a_send, a_recv, b_send, b_recv, far_sem,
+    plane_send, plane_recv, near_send, near_recv, far_send, far_recv, known_sem,
 ):
     n = dict(sizes)
     me = {axis: lax.axis_index(axis) for axis in ("gx", "gy", "gz")}
@@ -156,8 +156,9 @@
     load.start()
 
     barrier = pltpu.get_barrier_semaphore()
-    near = [device(gx=1), device(gx=-1), device(gy=1), device(gy=-1)]
-    near += [device(gx=i, gy=j) for i in (1, -1) for j in (1, -1)] + [device(gz=1)]
+    around = [(1, 1), (1, -1), (-1, 1), (-1, -1), (1, 0), (-1, 0), (0, 1), (0, -1)]
+    near = [device(gx=i, gy=j) for i, j in around] + [device(gz=1)]
+    near += [device(gx=i, gy=j, gz=1) for i, j in around]
     for where in near:
         pl.semaphore_signal(barrier, inc=1, device_id=where, device_id_type=MESH)
 
@@ -194,13 +195,13 @@
 
     load.wait()
     pl.semaphore_wait(barrier, len(near))
-    send(((nx - 2) * ny, 2 * ny), lay.xm, device(gx=1))
-    send((0, ny), lay.xp, device(gx=-1))
     for p in range(2):
         send(((nx - 2 + p) * ny + ny - 2, 2), lay.ym_xm + 2 * p, device(gx=1, gy=1))
         send(((nx - 2 + p) * ny, 1), lay.yp_xm + p, device(gx=1, gy=-1))
     send((ny - 2, 2), lay.ym_xp, device(gx=-1, gy=1))
     send((0, 1), lay.yp_xp, device(gx=-1, gy=-1))
+    send(((nx - 2) * ny, 2 * ny), lay.xm, device(gx=1))
+    send((0, ny), lay.xp, device(gx=-1))
     for p in range(nx):
         send((p * ny + ny - 2, 2), lay.ym_own + 2 * p, device(gy=1))
         send((p * ny, 1), lay.yp_own + p, device(gy=-1))
@@ -218,18 +219,22 @@
     core_own = to_core(0, 0, own)
     core_own.start()
 
-    def greet(step):
-        d = 2**step
-        for where in (device(gx=d), device(gx=-d), device(gy=d), device(gy=-d)):
-            pl.semaphore_signal(far_sem.at[step], inc=1, device_id=where, device_id_type=MESH)
-
-    far = 1
-    while 2**far < n["gx"] // 2 or 2**far <= n["gy"] // 2:
-        far += 1
-    for step in range(far):
-        greet(step)
-        if step < far - 1:
-            pl.semaphore_wait(far_sem.at[step], 4)
+    rounds = {
+        "gx": max(1, math.ceil(math.log2(n["gx"] / 2))), "gy": max(1, math.ceil(math.log2(n["gy"] / 2)))
+    }
+    last = max(rounds.values())
+
+    def greeted(step):
+        return [axis for axis in ("gx", "gy") if step < rounds[axis]]
+
+    for step in range(last):
+        for axis in greeted(step):
+            for d in (2**step, -(2**step)):
+                pl.semaphore_signal(
+                    known_sem.at[step], inc=1, device_id=device(**{axis: d}), device_id_type=MESH
+                )
+        if step < last - 1:
+            pl.semaphore_wait(known_sem.at[step], 2 * len(greeted(step)))
 
     for copy in sends:
         copy.wait()
@@ -348,45 +353,66 @@
             product = part * (part if c < 3 else ext[c, :own])
             for k in range(own // 8):
                 total = total + product[8 * k : 8 * k + 8]
-        sums.append(jnp.sum(total, axis=0, keepdims=True))
-    totals = jnp.concatenate(sums, axis=0)
-
-    pl.semaphore_wait(far_sem.at[far - 1], 4)
-
-    def exchange(totals, partners, sending, receiving, send_sems, recv_sems):
-        sending[...] = totals
-        copies = []
-        for slot, where in enumerate(partners):
-            copy = pltpu.make_async_remote_copy(
-                src_ref=sending,
-                dst_ref=receiving.at[slot],
-                send_sem=send_sems.at[slot],
-                recv_sem=recv_sems.at[slot],
-                device_id=where,
-                device_id_type=MESH,
-            )
-            copy.start()
-            copies.append(copy)
-        for copy in copies:
-            copy.wait_recv()
-        return totals + jnp.sum(receiving[...], axis=0), copies
-
-    half = n["gx"] // 2
-    order = [k for d in range(1, half + 1) for k in sorted({d, n["gx"] - d})]
-    totals, copies_a = exchange(
-        totals, [device(gx=k) for k in order], send_a, recv_a, a_send, a_recv
-    )
+        sums.append(total + pltpu.roll(total, nz // 2, 1))
+    lane = lax.broadcasted_iota(jnp.int32, (8, nz), 1)
+    folded = jnp.sum(jnp.where(lane < nz // 2, sums[0], sums[1]), axis=0, keepdims=True)
+    own_row[...] = folded
+
+    def row_to(source, target, slot, send_sems, recv_sems, where):
+        copy = pltpu.make_async_remote_copy(
+            src_ref=source,
+            dst_ref=target.at[slot : slot + 1],
+            send_sem=send_sems.at[slot],
+            recv_sem=recv_sems.at[slot],
+            device_id=where,
+            device_id_type=MESH,
+        )
+        copy.start()
+        return copy
+
     half = n["gy"] // 2
-    order = [k for d in range(half, 0, -1) for k in sorted({d, n["gy"] - d})] + [0]
-    partners = []
-    for k in order:
-        partners.append(device(gy=k, gz=1))
-        if k:
-            partners.append(device(gy=k))
-    totals, copies_b = exchange(totals, partners, send_b, recv_b, b_send, b_recv)
-    totals_ref[...] = totals
-    for copy in copies_a + copies_b:
+    if rounds["gy"] >= last:
+        pl.semaphore_wait(known_sem.at[last - 1], 2 * len(greeted(last - 1)))
+    in_plane, in_near = [], []
+    for k in [k for d in range(half, 0, -1) for k in sorted({d, n["gy"] - d})] + [0]:
+        for i in beside(n["gx"]):
+            for core in (1, 0):
+                where = device(gx=i, gy=k, gz=core)
+                in_near.append(
+                    row_to(own_row, near_rows, len(in_near), near_send, near_recv, where)
+                )
+        for core in (1, 0):
+            if k or core:
+                where = device(gy=k, gz=core)
+                in_plane.append(
+                    row_to(own_row, plane_rows, len(in_plane), plane_send, plane_recv, where)
+                )
+    for copy in in_plane:
+        copy.wait_recv()
+    plane_total = folded + jnp.sum(plane_rows[...], axis=0, keepdims=True)
+    plane_row[...] = plane_total
+    if rounds["gy"] < last:
+        pl.semaphore_wait(known_sem.at[last - 1], 2 * len(greeted(last - 1)))
+    in_far = [
+        row_to(plane_row, far_rows, slot, far_send, far_recv, device(gx=k))
+        for slot, k in enumerate(beyond(n["gx"]))
+    ]
+    for copy in in_near + in_far:
+        copy.wait_recv()
+    total = plane_total + jnp.sum(near_rows[...], axis=0, keepdims=True)
+    if in_far:
+        total = total + jnp.sum(far_rows[...], axis=0, keepdims=True)
+    totals_ref[...] = total
+    for copy in in_plane + in_near + in_far:
         copy.wait_send()
+
+
+def beside(size):
+    return sorted({1, size - 1})
+
+
+def beyond(size):
+    return [k for k in range(1, size) if k not in beside(size)]
 
 
 def finish(entries, out, totals, residual, tangent, stats, held, sems):
@@ -397,10 +423,12 @@
     ]
     for copy in copies:
         copy.start()
-    means = jnp.sum(totals[...], axis=1, keepdims=True) / entries
-    root = jnp.sqrt(means + root_eps)
-    held[0] = root[0, 0]
-    held[1] = means[1, 0]
+    row = totals[...]
+    first = lax.broadcasted_iota(jnp.int32, row.shape, 1) < row.shape[1] // 2
+    squares = jnp.sum(jnp.where(first, row, 0.0), axis=1, keepdims=True) / entries
+    curvature = jnp.sum(jnp.where(first, 0.0, row), axis=1, keepdims=True) / entries
+    held[0] = jnp.sqrt(squares + root_eps)[0, 0]
+    held[1] = curvature[0, 0]
     copies.append(pltpu.make_async_copy(held, stats, sems.at[2]))
     copies[-1].start()
     for copy in copies:
@@ -419,13 +447,14 @@
         vmem = pl.BlockSpec(memory_space=pltpu.VMEM)
         halos = 2 + 2 * nx + 6
         own = lay.own
-        n_a, n_b = n["gx"] - 1, n["gy"] * n["gz"] - 1
+        plane = n["gy"] * n["gz"]
+        near, far = plane * len(beside(n["gx"])), len(beyond(n["gx"]))
         dma = pltpu.SemaphoreType.DMA
         out, totals = pl.pallas_call(
             functools.partial(kernel, lay, sizes),
             out_shape=(
                 pltpu.VMEM((6 * own, nz), f32),
-                pltpu.VMEM((2, nz), f32),
+                pltpu.VMEM((1, nz), f32),
             ),
             in_specs=[hbm] * 8,
             out_specs=(vmem, vmem),
@@ -438,20 +467,23 @@
                 pltpu.VMEM((2, 3, 3, lay.points, 256), f32),
                 pltpu.VMEM((6, 3, lay.points, lay.lanes), f32),
                 pltpu.VMEM((2, 2, 6 * own, lay.lanes), bf16),
-                pltpu.VMEM((2, nz), f32),
-                pltpu.VMEM((n_a, 2, nz), f32),
-                pltpu.VMEM((2, nz), f32),
-                pltpu.VMEM((n_b, 2, nz), f32),
+                pltpu.VMEM((1, nz), f32),
+                pltpu.VMEM((1, nz), f32),
+                pltpu.VMEM((plane - 1, nz), f32),
+                pltpu.VMEM((near, nz), f32),
+                pltpu.VMEM((max(far, 1), nz), f32),
                 dma,
                 dma((7,)),
                 dma((halos,)),
                 dma((halos,)),
                 dma((2,)),
                 dma((2,)),
-                dma((n_a,)),
-                dma((n_a,)),
-                dma((n_b,)),
-                dma((n_b,)),
+                dma((plane - 1,)),
+                dma((plane - 1,)),
+                dma((near,)),
+                dma((near,)),
+                dma((max(far, 1),)),
+                dma((max(far, 1),)),
                 pltpu.SemaphoreType.REGULAR((8,)),
             ],
             compiler_params=pltpu.CompilerParams(

time: 67.6 us -> 65.9 us (0.975)
  Pallas kernels: 66.9 us -> 65 us
    pallas_call x1, Pallas kernels: 66.2 us -> 64.3 us  [local(): pl.pallas_call(functools.partial(kernel, lay, sizes), out_shape=(pltpu.VM...]
where the time goes in v3:
time: 65.9 us; the launch traced here: 65.6 us
  Pallas kernels  65 us (99%)
    pallas_call x1, Pallas kernels, local(): pl.pallas_call(functools.partial(kernel, lay, sizes), out_shape=(pltpu.VM...  64.3 us

profile of v3, /device:TPU:65, one launch (start us, length us, event | category | flops | bytes accessed | tf_op | source)
XLA Modules:
  0.0 65.6 jit_solution(13410028383930877684)
XLA Ops:
  0.6 64.3 %cell.1 = (f32[192,128]{1,0:T(8,128)S(1)}, f32[1,128]{1,0:T(1,128)S(1)}) custom-call(f32[6,32,128]{2,1,0:T(8,128)} %bitcast.3, f32[3,3]{1,0:T(4,128)} %strain_h.1, f32[2]{0:T(128)} %material_h.1, bf16[3,144,240]{2,1,0:T(8,128)(2,1)} %constant.10.clone.forward_h, bf16[3,64,144]{2,1,0:T(8,128)(2,1)} %constant.11.clone.back_h, ...), custom_call_target="tpu_custom_call" | custom-call | tf_op jit(solution)/shard_map/cell/pallas_call | solution.py:453
  64.9 0.7 %finish.1 = (f32[96,128]{1,0:T(8,128)}, f32[96,128]{1,0:T(8,128)}, f32[2]{0:T(128)}) custom-call(f32[192,128]{1,0:T(8,128)S(1)} %get-tuple-element.8.out, f32[1,128]{1,0:T(1,128)S(1)} %get-tuple-element.9.totals), custom_call_target="tpu_custom_call" | custom-call | tf_op jit(solution)/shard_map/finish/pallas_call | solution.py:496

commit v4 on v3

--- a/solution.py
+++ b/solution.py
@@ -225,13 +225,16 @@
     last = max(rounds.values())
 
     def greeted(step):
-        return [axis for axis in ("gx", "gy") if step < rounds[axis]]
+        shifts = [(axis, 2**step) for axis in ("gx", "gy") if step < rounds[axis]]
+        if step == last - 1 and step:
+            shifts.append(("gx", 2 ** (step - 1)))
+        return shifts
 
     for step in range(last):
-        for axis in greeted(step):
-            for d in (2**step, -(2**step)):
+        for axis, d in greeted(step):
+            for shift in (d, -d):
                 pl.semaphore_signal(
-                    known_sem.at[step], inc=1, device_id=device(**{axis: d}), device_id_type=MESH
+                    known_sem.at[step], inc=1, device_id=device(**{axis: shift}), device_id_type=MESH
                 )
         if step < last - 1:
             pl.semaphore_wait(known_sem.at[step], 2 * len(greeted(step)))
@@ -358,61 +361,59 @@
     folded = jnp.sum(jnp.where(lane < nz // 2, sums[0], sums[1]), axis=0, keepdims=True)
     own_row[...] = folded
 
-    def row_to(source, target, slot, send_sems, recv_sems, where):
-        copy = pltpu.make_async_remote_copy(
+    def row_to(source, target, slot, send_sem, recv_sem, where):
+        pltpu.make_async_remote_copy(
             src_ref=source,
             dst_ref=target.at[slot : slot + 1],
-            send_sem=send_sems.at[slot],
-            recv_sem=recv_sems.at[slot],
+            send_sem=send_sem,
+            recv_sem=recv_sem,
             device_id=where,
             device_id_type=MESH,
-        )
-        copy.start()
-        return copy
+        ).start()
+
+    def wait_rows(rows, sem):
+        pltpu.make_async_copy(rows, rows, sem).wait()
 
     half = n["gy"] // 2
-    if rounds["gy"] >= last:
-        pl.semaphore_wait(known_sem.at[last - 1], 2 * len(greeted(last - 1)))
-    in_plane, in_near = [], []
-    for k in [k for d in range(half, 0, -1) for k in sorted({d, n["gy"] - d})] + [0]:
-        for i in beside(n["gx"]):
-            for core in (1, 0):
-                where = device(gx=i, gy=k, gz=core)
-                in_near.append(
-                    row_to(own_row, near_rows, len(in_near), near_send, near_recv, where)
-                )
-        for core in (1, 0):
-            if k or core:
-                where = device(gy=k, gz=core)
-                in_plane.append(
-                    row_to(own_row, plane_rows, len(in_plane), plane_send, plane_recv, where)
-                )
-    for copy in in_plane:
-        copy.wait_recv()
+    order = [k for d in range(half, 0, -1) for k in sorted({d, n["gy"] - d})] + [0]
+    slot_near = slot_plane = 0
+    for planes in ((1, 0), (2, 3)):
+        if planes[0] == 2:
+            pl.semaphore_wait(known_sem.at[last - 1], 2 * len(greeted(last - 1)))
+        for k in order:
+            for i in planes:
+                for core in (1, 0):
+                    where = device(gx=i, gy=k, gz=core)
+                    if i in above(n["gx"]):
+                        row_to(own_row, near_rows, slot_near, near_send, near_recv, where)
+                        slot_near += 1
+                    elif i == 0 and (k or core):
+                        row_to(own_row, plane_rows, slot_plane, plane_send, plane_recv, where)
+                        slot_plane += 1
+    wait_rows(plane_rows, plane_recv)
     plane_total = folded + jnp.sum(plane_rows[...], axis=0, keepdims=True)
     plane_row[...] = plane_total
-    if rounds["gy"] < last:
-        pl.semaphore_wait(known_sem.at[last - 1], 2 * len(greeted(last - 1)))
-    in_far = [
+    far = beyond(n["gx"])
+    for slot, k in enumerate(far):
         row_to(plane_row, far_rows, slot, far_send, far_recv, device(gx=k))
-        for slot, k in enumerate(beyond(n["gx"]))
-    ]
-    for copy in in_near + in_far:
-        copy.wait_recv()
+    wait_rows(near_rows, near_recv)
     total = plane_total + jnp.sum(near_rows[...], axis=0, keepdims=True)
-    if in_far:
+    if far:
+        wait_rows(far_rows, far_recv)
         total = total + jnp.sum(far_rows[...], axis=0, keepdims=True)
     totals_ref[...] = total
-    for copy in in_plane + in_near + in_far:
-        copy.wait_send()
-
-
-def beside(size):
-    return sorted({1, size - 1})
+    wait_rows(plane_rows, plane_send)
+    wait_rows(near_rows, near_send)
+    if far:
+        wait_rows(far_rows, far_send)
+
+
+def above(size):
+    return range(1, min(size, 4))
 
 
 def beyond(size):
-    return [k for k in range(1, size) if k not in beside(size)]
+    return range(4, size)
 
 
 def finish(entries, out, totals, residual, tangent, stats, held, sems):
@@ -448,7 +449,7 @@
         halos = 2 + 2 * nx + 6
         own = lay.own
         plane = n["gy"] * n["gz"]
-        near, far = plane * len(beside(n["gx"])), len(beyond(n["gx"]))
+        near, far = plane * len(above(n["gx"])), len(beyond(n["gx"]))
         dma = pltpu.SemaphoreType.DMA
         out, totals = pl.pallas_call(
             functools.partial(kernel, lay, sizes),
@@ -478,12 +479,7 @@
                 dma((halos,)),
                 dma((2,)),
                 dma((2,)),
-                dma((plane - 1,)),
-                dma((plane - 1,)),
-                dma((near,)),
-                dma((near,)),
-                dma((max(far, 1),)),
-                dma((max(far, 1),)),
+                *[dma] * 6,
                 pltpu.SemaphoreType.REGULAR((8,)),
             ],
             compiler_params=pltpu.CompilerParams(

time: 65.9 us -> 64.6 us (0.980)
  Pallas kernels: 65 us -> 63.7 us
    pallas_call x1, Pallas kernels: 64.3 us -> 63 us  [local(): pl.pallas_call(functools.partial(kernel, lay, sizes), out_shape=(pltpu.VM...]
where the time goes in v4:
time: 64.6 us; the launch traced here: 64.3 us
  Pallas kernels  63.7 us (99%)
    pallas_call x1, Pallas kernels, local(): pl.pallas_call(functools.partial(kernel, lay, sizes), out_shape=(pltpu.VM...  63 us

profile of v4, /device:TPU:65, one launch (start us, length us, event | category | flops | bytes accessed | tf_op | source)
XLA Modules:
  0.0 64.3 jit_solution(10264059651702170796)
XLA Ops:
  0.6 63.0 %cell.1 = (f32[192,128]{1,0:T(8,128)S(1)}, f32[1,128]{1,0:T(1,128)S(1)}) custom-call(f32[6,32,128]{2,1,0:T(8,128)} %bitcast.3, f32[3,3]{1,0:T(4,128)} %strain_h.1, f32[2]{0:T(128)} %material_h.1, bf16[3,144,240]{2,1,0:T(8,128)(2,1)} %constant.10.clone.forward_h, bf16[3,64,144]{2,1,0:T(8,128)(2,1)} %constant.11.clone.back_h, ...), custom_call_target="tpu_custom_call" | custom-call | tf_op jit(solution)/shard_map/cell/pallas_call | solution.py:454
  63.6 0.7 %finish.1 = (f32[96,128]{1,0:T(8,128)}, f32[96,128]{1,0:T(8,128)}, f32[2]{0:T(128)}) custom-call(f32[192,128]{1,0:T(8,128)S(1)} %get-tuple-element.8.out, f32[1,128]{1,0:T(1,128)S(1)} %get-tuple-element.9.totals), custom_call_target="tpu_custom_call" | custom-call | tf_op jit(solution)/shard_map/finish/pallas_call | solution.py:492

commit v5 on v4

--- a/solution.py
+++ b/solution.py
@@ -38,10 +38,11 @@
         self.xm = self.own
         self.xp = self.xm + 2 * ny
         self.ym_own = self.xp + ny
-        self.ym_xm = self.ym_own + 2 * nx
+        self.yp_own = self.ym_own + 2 * nx
+        self.corners = self.yp_own + nx
+        self.ym_xm = self.corners
         self.ym_xp = self.ym_xm + 4
-        self.yp_own = self.ym_xp + 2
-        self.yp_xm = self.yp_own + nx
+        self.yp_xm = self.ym_xp + 2
         self.yp_xp = self.yp_xm + 2
         self.used = self.yp_xp + 1
         self.rows = ceil_to(self.used, 16)
@@ -112,7 +113,7 @@
                     z_back[kind, column, z] += tz[q3, a3] * weights[q3]
                 along_z[kind, k, column] += tz[q3, a3]
     fh, fl = split_np(forward)
-    forward = np.concatenate([fh, fh, fl], axis=2)
+    forward = np.concatenate([fh, fh, fl], axis=2).reshape(3 * lay.points, 3 * lay.rows)
     bh, bl = split_np(back)
     back = np.concatenate([bh, bl], axis=1)
     first = np.concatenate(along_z[:, : lay.nz, :128], axis=1)
@@ -174,17 +175,29 @@
     for copy in constants:
         copy.start()
     if rows > lay.used:
-        ext[:, lay.used :, :] = jnp.zeros((6, rows - lay.used, nz), f32)
+        for target in (ext, extp):
+            target[:, lay.used :, :] = jnp.zeros((6, rows - lay.used, nz), f32)
+
+    def along_first(nodes):
+        high, low = split(nodes)
+        weights = first[0:nz]
+        return dot(
+            jnp.concatenate([high, low], axis=1), jnp.concatenate([weights, weights], axis=0)
+        ) + dot(high, first[nz:])
+
+    def along_second(mine, other):
+        high, low = split(jnp.concatenate([mine, other], axis=1))
+        return dot(high, second[0]) + dot(low, second[0]) + dot(high, second[1])
 
     count = [0]
     sends = []
 
-    def send(source, target, where):
+    def send(source, target, where, into=ext):
         i = count[0]
         count[0] += 1
         copy = pltpu.make_async_remote_copy(
             src_ref=ext.at[:, source[0] : source[0] + source[1], :],
-            dst_ref=ext.at[:, target : target + source[1], :],
+            dst_ref=into.at[:, target : target + source[1], :],
             send_sem=halo_send.at[i],
             recv_sem=halo_recv.at[i],
             device_id=where,
@@ -195,11 +208,13 @@
 
     load.wait()
     pl.semaphore_wait(barrier, len(near))
-    for p in range(2):
-        send(((nx - 2 + p) * ny + ny - 2, 2), lay.ym_xm + 2 * p, device(gx=1, gy=1))
-        send(((nx - 2 + p) * ny, 1), lay.yp_xm + p, device(gx=1, gy=-1))
-    send((ny - 2, 2), lay.ym_xp, device(gx=-1, gy=1))
-    send((0, 1), lay.yp_xp, device(gx=-1, gy=-1))
+    for core, into in enumerate((ext, extp)):
+        for p in range(2):
+            start = (nx - 2 + p) * ny
+            send((start + ny - 2, 2), lay.ym_xm + 2 * p, device(gx=1, gy=1, gz=core), into)
+            send((start, 1), lay.yp_xm + p, device(gx=1, gy=-1, gz=core), into)
+        send((ny - 2, 2), lay.ym_xp, device(gx=-1, gy=1, gz=core), into)
+        send((0, 1), lay.yp_xp, device(gx=-1, gy=-1, gz=core), into)
     send(((nx - 2) * ny, 2 * ny), lay.xm, device(gx=1))
     send((0, ny), lay.xp, device(gx=-1))
     for p in range(nx):
@@ -230,35 +245,65 @@
             shifts.append(("gx", 2 ** (step - 1)))
         return shifts
 
-    for step in range(last):
+    def greet(step):
         for axis, d in greeted(step):
             for shift in (d, -d):
                 pl.semaphore_signal(
                     known_sem.at[step], inc=1, device_id=device(**{axis: shift}), device_id_type=MESH
                 )
-        if step < last - 1:
-            pl.semaphore_wait(known_sem.at[step], 2 * len(greeted(step)))
-
-    for copy in sends:
-        copy.wait()
-    core_halo = to_core(1, own, rows)
-    core_halo.start()
+
+    def next_round(step):
+        pl.semaphore_wait(known_sem.at[step], 2 * len(greeted(step)))
+        greet(step + 1)
+
+    here, top = me["gx"], n["gx"] - 1
+    at_end = (here >= top - 2) | (here <= 1)
+    greet(0)
+    for step in range(last - 2):
+        next_round(step)
+    if last > 1:
+        @pl.when(at_end)
+        def _():
+            next_round(last - 2)
+
     for copy in constants:
         copy.wait()
-
-    def to_points(tile, z):
-        high, low = split(z)
-        for pair in range(3):
+    own_nodes = ext[:, :own].reshape(6 * own, nz)
+    z_own = along_first(own_nodes)
+    core_own.wait()
+    z_own_second = along_second(own_nodes, extp[:, :own].reshape(6 * own, nz))
+    for copy in sends[12:]:
+        copy.wait()
+    core_halo = to_core(1, own, lay.corners)
+    core_halo.start()
+    for copy in sends[:12]:
+        copy.wait()
+
+    def to_points(tile, z_mine, z_halo):
+        mine, halo = split(z_mine), split(z_halo)
+        rest = rows - own
+
+        def one(pair):
             parts = []
             for kind in range(2):
                 sides = []
+                lanes = slice(kind * 128, kind * 128 + 128)
                 for c in (2 * pair, 2 * pair + 1):
-                    at = (slice(c * rows, c * rows + rows), slice(kind * 128, kind * 128 + 128))
-                    sides.append(jnp.concatenate([high[at], low[at], high[at]], axis=0))
+                    high, low = (
+                        jnp.concatenate(
+                            [a[c * own : c * own + own, lanes], b[c * rest : c * rest + rest, lanes]],
+                            axis=0,
+                        )
+                        for a, b in zip(mine, halo)
+                    )
+                    sides.append(jnp.concatenate([high, low, high], axis=0))
                 parts.append(jnp.concatenate(sides, axis=1))
-            grads[tile, pair, 0] = dot(forward[0], parts[0])
-            grads[tile, pair, 1] = dot(forward[1], parts[0])
-            grads[tile, pair, 2] = dot(forward[2], parts[1])
+            both = dot(forward[: 2 * lay.points], parts[0])
+            grads[tile, pair, 0] = both[: lay.points]
+            grads[tile, pair, 1] = both[lay.points :]
+            grads[tile, pair, 2] = dot(forward[2 * lay.points :], parts[1])
+
+        return one
 
     shear, lame = material[0], material[1]
     ratio = lame / shear
@@ -266,15 +311,20 @@
         [strain[i, j] + (1.0 if i == j else 0.0) for j in range(3)] for i in range(3)
     ]
 
+    def side(c):
+        return slice((c % 2) * 128, (c % 2) * 128 + 128)
+
     def stresses(tile):
         def points(i, carry):
             for half in range(2):
-                block = pl.ds(pl.multiple_of(i * 16 + half * 8, 8), 8)
+                if isinstance(i, int):
+                    block = slice(i * 16 + half * 8, i * 16 + half * 8 + 8)
+                else:
+                    block = pl.ds(pl.multiple_of(i * 16 + half * 8, 8), 8)
 
                 def gradient(c, along):
-                    return grads[tile, c // 2, along, block, (c % 2) * 128 : (c % 2) * 128 + 128]
-
-                lanes = slice(tile * 128, tile * 128 + 128)
+                    return grads[tile, c // 2, along, block, side(c)]
+
                 f = [[gradient(r, c) + shift[r][c] for c in range(3)] for r in range(3)]
                 dv = [[gradient(3 + r, c) for c in range(3)] for r in range(3)]
                 cof = [
@@ -289,9 +339,10 @@
                 inverse = 1.0 / det
                 g = [[cof[r][c] * inverse for c in range(3)] for r in range(3)]
                 pressure = ratio * jnp.log(det) - 1.0
+                soft = -pressure
                 for r in range(3):
                     for c in range(3):
-                        flux[r, c, block, lanes] = f[r][c] + pressure * g[r][c]
+                        flux[tile, r // 2, c, block, side(r)] = f[r][c] + pressure * g[r][c]
                 m = [
                     [
                         g[r][0] * dv[c][0] + g[r][1] * dv[c][1] + g[r][2] * dv[c][2]
@@ -301,49 +352,50 @@
                 ]
                 trace = ratio * (m[0][0] + m[1][1] + m[2][2])
                 w = [
-                    [
-                        trace - pressure * m[r][c] if r == c else -(pressure * m[r][c])
-                        for c in range(3)
-                    ]
+                    [trace + soft * m[r][c] if r == c else soft * m[r][c] for c in range(3)]
                     for r in range(3)
                 ]
                 for r in range(3):
                     for c in range(3):
-                        flux[3 + r, c, block, lanes] = dv[r][c] + (
+                        flux[tile, (3 + r) // 2, c, block, side(3 + r)] = dv[r][c] + (
                             w[r][0] * g[0][c] + w[r][1] * g[1][c] + w[r][2] * g[2][c]
                         )
             return carry
 
-        lax.fori_loop(0, lay.points // 16, points, 0)
-
-    nodes = ext[...].reshape(6 * rows, nz)
-    high, low = split(nodes)
-    weights = first[0:nz]
-    z = dot(
-        jnp.concatenate([high, low], axis=1), jnp.concatenate([weights, weights], axis=0)
-    ) + dot(high, first[nz:])
-    to_points(0, z)
-    stresses(0)
-
-    core_own.wait()
-    core_halo.wait()
-    nodes = jnp.concatenate([nodes, extp[...].reshape(6 * rows, nz)], axis=1)
-    high, low = split(nodes)
-    z = dot(high, second[0]) + dot(low, second[0]) + dot(high, second[1])
-    to_points(1, z)
-    stresses(1)
-
-    for c in range(6):
+        return points
+
+    rest = 6 * (rows - own)
+    halo_nodes = ext[:, own:].reshape(rest, nz)
+    def back_pair(tile, pair):
         def plane(kind, along):
-            high, low = split(flux[c, along])
+            high, low = split(flux[tile, pair, along])
             both = dot(back[kind], high)
             return both[:own] + both[own:] + dot(back[kind, :own], low)
 
-        at = slice(c * own, c * own + own)
         for kind, part in enumerate((plane(0, 0) + plane(1, 1), plane(2, 2))):
-            high, low = split(part)
-            middle[kind, 0, at] = high
-            middle[kind, 1, at] = low
+            for hl, piece in enumerate(split(part)):
+                for c in (2 * pair, 2 * pair + 1):
+                    at = slice(c * own, c * own + own)
+                    middle[kind, hl, at, tile * 128 : tile * 128 + 128] = piece[:, side(c)]
+
+    points_of = to_points(0, z_own, along_first(halo_nodes))
+    for pair in range(3):
+        points_of(pair)
+    core_halo.wait()
+    points_of = to_points(1, z_own_second, along_second(halo_nodes, extp[:, own:].reshape(rest, nz)))
+    blocks = lay.points // 16
+    for tile in range(2):
+        stress = stresses(tile)
+        for i in range(blocks):
+            if i % (blocks // 3) == 0:
+                pair = i // (blocks // 3)
+                if tile == 0:
+                    points_of(pair)
+                else:
+                    back_pair(0, pair)
+            stress(i, 0)
+    for pair in range(3):
+        back_pair(1, pair)
     result = dot(middle[0, 1], z_back[0, :, :nz]) + dot(middle[1, 1], z_back[1, :, :nz])
     both = dot(middle[0, 0], z_back[0]) + dot(middle[1, 0], z_back[1])
     result = (result + both[:, :nz] + both[:, nz:]) * shear
@@ -376,6 +428,11 @@
 
     half = n["gy"] // 2
     order = [k for d in range(half, 0, -1) for k in sorted({d, n["gy"] - d})] + [0]
+    if last > 1:
+        @pl.when(jnp.logical_not(at_end))
+        def _():
+            next_round(last - 2)
+
     slot_near = slot_plane = 0
     for planes in ((1, 0), (2, 3)):
         if planes[0] == 2:
@@ -446,7 +503,7 @@
         consts = [jnp.asarray(m) for m in matrices(lay)]
         hbm = pl.BlockSpec(memory_space=pltpu.HBM)
         vmem = pl.BlockSpec(memory_space=pltpu.VMEM)
-        halos = 2 + 2 * nx + 6
+        halos = 2 + 2 * nx + 12
         own = lay.own
         plane = n["gy"] * n["gz"]
         near, far = plane * len(above(n["gx"])), len(beyond(n["gx"]))
@@ -466,7 +523,7 @@
                 pltpu.SMEM(material.shape, f32),
                 *[pltpu.VMEM(m.shape, bf16) for m in consts],
                 pltpu.VMEM((2, 3, 3, lay.points, 256), f32),
-                pltpu.VMEM((6, 3, lay.points, lay.lanes), f32),
+                pltpu.VMEM((2, 3, 3, lay.points, 256), f32),
                 pltpu.VMEM((2, 2, 6 * own, lay.lanes), bf16),
                 pltpu.VMEM((1, nz), f32),
                 pltpu.VMEM((1, nz), f32),

time: 64.6 us -> 64.1 us (level)
  no operation moved by 1% of the time
where the time goes in v5:
time: 64.1 us; the launch traced here: 63.9 us
  Pallas kernels  63.3 us (99%)
    pallas_call x1, Pallas kernels, local(): pl.pallas_call(functools.partial(kernel, lay, sizes), out_shape=(pltpu.VM...  62.6 us

profile of v5, /device:TPU:65, one launch (start us, length us, event | category | flops | bytes accessed | tf_op | source)
XLA Modules:
  0.0 63.9 jit_solution(11948542837823614937)
XLA Ops:
  0.6 62.6 %cell.1 = (f32[192,128]{1,0:T(8,128)S(1)}, f32[1,128]{1,0:T(1,128)S(1)}) custom-call(f32[6,32,128]{2,1,0:T(8,128)} %bitcast.3, f32[3,3]{1,0:T(4,128)} %strain_h.1, f32[2]{0:T(128)} %material_h.1, bf16[432,240]{1,0:T(8,128)(2,1)} %constant.10.clone.forward_h, bf16[3,64,144]{2,1,0:T(8,128)(2,1)} %constant.11.clone.back_h, ...), custom_call_target="tpu_custom_call" | custom-call | tf_op jit(solution)/shard_map/cell/pallas_call | solution.py:511
  63.3 0.7 %finish.1 = (f32[96,128]{1,0:T(8,128)}, f32[96,128]{1,0:T(8,128)}, f32[2]{0:T(128)}) custom-call(f32[192,128]{1,0:T(8,128)S(1)} %get-tuple-element.8.out, f32[1,128]{1,0:T(1,128)S(1)} %get-tuple-element.9.totals), custom_call_target="tpu_custom_call" | custom-call | tf_op jit(solution)/shard_map/finish/pallas_call | solution.py:549

commit v6 on v5

--- a/solution.py
+++ b/solution.py
@@ -268,20 +268,26 @@
 
     for copy in constants:
         copy.wait()
-    own_nodes = ext[:, :own].reshape(6 * own, nz)
-    z_own = along_first(own_nodes)
+    late = lay.corners // 16 * 16
+    bounds = [0, own, late, rows]
+    sizes_of = [stop - start for start, stop in zip(bounds, bounds[1:])]
+
+    def nodes(ref, i):
+        return ref[:, bounds[i] : bounds[i + 1]].reshape(6 * sizes_of[i], nz)
+
+    z_first = [along_first(nodes(ext, 0))]
     core_own.wait()
-    z_own_second = along_second(own_nodes, extp[:, :own].reshape(6 * own, nz))
+    z_second = [along_second(nodes(ext, 0), nodes(extp, 0))]
     for copy in sends[12:]:
         copy.wait()
     core_halo = to_core(1, own, lay.corners)
     core_halo.start()
+    z_first.append(along_first(nodes(ext, 1)))
     for copy in sends[:12]:
         copy.wait()
 
-    def to_points(tile, z_mine, z_halo):
-        mine, halo = split(z_mine), split(z_halo)
-        rest = rows - own
+    def to_points(tile, pieces):
+        parts_of = [split(z) for z in pieces]
 
         def one(pair):
             parts = []
@@ -291,10 +297,13 @@
                 for c in (2 * pair, 2 * pair + 1):
                     high, low = (
                         jnp.concatenate(
-                            [a[c * own : c * own + own, lanes], b[c * rest : c * rest + rest, lanes]],
+                            [
+                                part[hl][c * size : c * size + size, lanes]
+                                for part, size in zip(parts_of, sizes_of)
+                            ],
                             axis=0,
                         )
-                        for a, b in zip(mine, halo)
+                        for hl in range(2)
                     )
                     sides.append(jnp.concatenate([high, low, high], axis=0))
                 parts.append(jnp.concatenate(sides, axis=1))
@@ -364,8 +373,6 @@
 
         return points
 
-    rest = 6 * (rows - own)
-    halo_nodes = ext[:, own:].reshape(rest, nz)
     def back_pair(tile, pair):
         def plane(kind, along):
             high, low = split(flux[tile, pair, along])
@@ -378,22 +385,22 @@
                     at = slice(c * own, c * own + own)
                     middle[kind, hl, at, tile * 128 : tile * 128 + 128] = piece[:, side(c)]
 
-    points_of = to_points(0, z_own, along_first(halo_nodes))
+    z_first.append(along_first(nodes(ext, 2)))
+    points_of = to_points(0, z_first)
     for pair in range(3):
         points_of(pair)
+    blocks = lay.points // 16
+    for i in range(blocks):
+        stresses(0)(i, 0)
     core_halo.wait()
-    points_of = to_points(1, z_own_second, along_second(halo_nodes, extp[:, own:].reshape(rest, nz)))
-    blocks = lay.points // 16
-    for tile in range(2):
-        stress = stresses(tile)
-        for i in range(blocks):
-            if i % (blocks // 3) == 0:
-                pair = i // (blocks // 3)
-                if tile == 0:
-                    points_of(pair)
-                else:
-                    back_pair(0, pair)
-            stress(i, 0)
+    z_second += [along_second(nodes(ext, i), nodes(extp, i)) for i in (1, 2)]
+    points_of = to_points(1, z_second)
+    for pair in range(3):
+        points_of(pair)
+    for i in range(blocks):
+        if i % (blocks // 3) == 0:
+            back_pair(0, i // (blocks // 3))
+        stresses(1)(i, 0)
     for pair in range(3):
         back_pair(1, pair)
     result = dot(middle[0, 1], z_back[0, :, :nz]) + dot(middle[1, 1], z_back[1, :, :nz])

time: 64.1 us -> 63.9 us (level)
  no operation moved by 1% of the time
where the time goes in v6:
time: 63.9 us; the launch traced here: 63.7 us
  Pallas kernels  63.1 us (99%)
  between operations  0.64 us (1%)
    pallas_call x1, Pallas kernels, local(): pl.pallas_call(functools.partial(kernel, lay, sizes), out_shape=(pltpu.VM...  62.4 us

profile of v6, /device:TPU:65, one launch (start us, length us, event | category | flops | bytes accessed | tf_op | source)
XLA Modules:
  0.0 63.7 jit_solution(17866058249467463526)
XLA Ops:
  0.6 62.4 %cell.1 = (f32[192,128]{1,0:T(8,128)S(1)}, f32[1,128]{1,0:T(1,128)S(1)}) custom-call(f32[6,32,128]{2,1,0:T(8,128)} %bitcast.3, f32[3,3]{1,0:T(4,128)} %strain_h.1, f32[2]{0:T(128)} %material_h.1, bf16[432,240]{1,0:T(8,128)(2,1)} %constant.10.clone.forward_h, bf16[3,64,144]{2,1,0:T(8,128)(2,1)} %constant.11.clone.back_h, ...), custom_call_target="tpu_custom_call" | custom-call | tf_op jit(solution)/shard_map/cell/pallas_call | solution.py:518
  63.0 0.7 %finish.1 = (f32[96,128]{1,0:T(8,128)}, f32[96,128]{1,0:T(8,128)}, f32[2]{0:T(128)}) custom-call(f32[192,128]{1,0:T(8,128)S(1)} %get-tuple-element.8.out, f32[1,128]{1,0:T(1,128)S(1)} %get-tuple-element.9.totals), custom_call_target="tpu_custom_call" | custom-call | tf_op jit(solution)/shard_map/finish/pallas_call | solution.py:556

commit v7 on v6

--- a/solution.py
+++ b/solution.py
@@ -157,9 +157,9 @@
     load.start()
 
     barrier = pltpu.get_barrier_semaphore()
-    around = [(1, 1), (1, -1), (-1, 1), (-1, -1), (1, 0), (-1, 0), (0, 1), (0, -1)]
-    near = [device(gx=i, gy=j) for i, j in around] + [device(gz=1)]
-    near += [device(gx=i, gy=j, gz=1) for i, j in around]
+    beside = [(i, j) for i in (-1, 1) for j in (1, -1, 0)]
+    near = [device(gx=i, gy=j, gz=core) for i, j in beside for core in (0, 1)]
+    near += [device(gy=j, gz=core) for j in (1, -1) for core in (0, 1)] + [device(gz=1)]
     for where in near:
         pl.semaphore_signal(barrier, inc=1, device_id=where, device_id_type=MESH)
 
@@ -213,9 +213,10 @@
             start = (nx - 2 + p) * ny
             send((start + ny - 2, 2), lay.ym_xm + 2 * p, device(gx=1, gy=1, gz=core), into)
             send((start, 1), lay.yp_xm + p, device(gx=1, gy=-1, gz=core), into)
+    send(((nx - 2) * ny, 2 * ny), lay.xm, device(gx=1))
+    for core, into in enumerate((ext, extp)):
         send((ny - 2, 2), lay.ym_xp, device(gx=-1, gy=1, gz=core), into)
         send((0, 1), lay.yp_xp, device(gx=-1, gy=-1, gz=core), into)
-    send(((nx - 2) * ny, 2 * ny), lay.xm, device(gx=1))
     send((0, ny), lay.xp, device(gx=-1))
     for p in range(nx):
         send((p * ny + ny - 2, 2), lay.ym_own + 2 * p, device(gy=1))
@@ -278,12 +279,12 @@
     z_first = [along_first(nodes(ext, 0))]
     core_own.wait()
     z_second = [along_second(nodes(ext, 0), nodes(extp, 0))]
-    for copy in sends[12:]:
+    for copy in sends[8:9] + sends[13:]:
         copy.wait()
     core_halo = to_core(1, own, lay.corners)
     core_halo.start()
     z_first.append(along_first(nodes(ext, 1)))
-    for copy in sends[:12]:
+    for copy in sends[:8] + sends[9:13]:
         copy.wait()
 
     def to_points(tile, pieces):

time: 63.9 us -> 64 us (level)
  no operation moved by 1% of the time
where the time goes in v7:
time: 64 us; the launch traced here: 63.9 us
  Pallas kernels  63.2 us (99%)
  between operations  0.64 us (1%)
    pallas_call x1, Pallas kernels, local(): pl.pallas_call(functools.partial(kernel, lay, sizes), out_shape=(pltpu.VM...  62.6 us

profile of v7, /device:TPU:65, one launch (start us, length us, event | category | flops | bytes accessed | tf_op | source)
XLA Modules:
  0.0 63.9 jit_solution(2199008142170193899)
XLA Ops:
  0.6 62.6 %cell.1 = (f32[192,128]{1,0:T(8,128)S(1)}, f32[1,128]{1,0:T(1,128)S(1)}) custom-call(f32[6,32,128]{2,1,0:T(8,128)} %bitcast.3, f32[3,3]{1,0:T(4,128)} %strain_h.1, f32[2]{0:T(128)} %material_h.1, bf16[432,240]{1,0:T(8,128)(2,1)} %constant.10.clone.forward_h, bf16[3,64,144]{2,1,0:T(8,128)(2,1)} %constant.11.clone.back_h, ...), custom_call_target="tpu_custom_call" | custom-call | tf_op jit(solution)/shard_map/cell/pallas_call | solution.py:519
  63.2 0.7 %finish.1 = (f32[96,128]{1,0:T(8,128)}, f32[96,128]{1,0:T(8,128)}, f32[2]{0:T(128)}) custom-call(f32[192,128]{1,0:T(8,128)S(1)} %get-tuple-element.8.out, f32[1,128]{1,0:T(1,128)S(1)} %get-tuple-element.9.totals), custom_call_target="tpu_custom_call" | custom-call | tf_op jit(solution)/shard_map/finish/pallas_call | solution.py:557
